TPU v7x, 32 devices: a whole 2x2x4 slice. The times are simulated.
32 devices in a mesh: row: 16 (over z, y, x), grp: 2 (over core).
Axes of the slice: x: 2, y: 2, z: 4, core: 2. Of those that a mesh axis runs over, the one named last changes fastest.
Arguments:
- features: float32 [131072, 256], P(('row', 'grp')), may hold values from -6 to 6
- session: int32 [131072], P(('row', 'grp')), may hold values from 0 to 1023, never falling along the last dimension, each value on 1 to 65536 neighbouring positions
- owner_map: int32 [32, 64], P(('row', 'grp')), may hold values from 0 to 15, as said below
Outputs:
- received: bfloat16 [4096, 64, 256], P(('row', 'grp'))
Inputs may be any that keep to these rules, and one draw needn't show every extreme that they name: session numbers never fall along the rows; each session covers 1 to 65536 consecutive rows. `owner_map`: no owner is named by more than 8 of the blocks of one group of 64.
All inputs are finite; a program needn't handle non-finite values.
Results may differ from a plain program's by a relative error of at most 0.001.
Values may be sent and summed in bfloat16 or wider, within the bound.
No kernel may reach another device: no remote copies, remote signals or barrier semaphores. Data moves between devices by JAX's collectives and lax.ppermute only.
A program may use at most 128 MiB of HBM per device.

v0:
```python
import jax
import jax.numpy as jnp
from jax import lax
from jax.sharding import PartitionSpec as P


def prefix(array, axis, combine, identity):
    size, here = (lax.axis_size(axis), lax.axis_index(axis))
    everything = jax.tree.map(lambda part: lax.all_gather(part, axis), array)
    start = jax.tree.map(
        lambda part, zero: jnp.broadcast_to(jnp.asarray(zero, part.dtype), part.shape),
        array,
        identity,
    )

    def turn(k, before):
        reached = k < here
        new = combine(before, jax.tree.map(lambda part: part[k], everything))
        return jax.tree.map(lambda a, b: jnp.where(reached, a, b), new, before)

    return lax.fori_loop(0, size, turn, start)


def local_sums(features, session, block_count):
    rows_dev, feature_width = features.shape
    block_rows = rows_dev // block_count
    grouped = features.reshape(block_count, block_rows, feature_width)
    grouped_ids = session.reshape(block_count, block_rows)
    position = jnp.arange(block_rows)
    same_mask = (
        (grouped_ids[:, :, None] == grouped_ids[:, None, :])
        & (position[None, None, :] <= position[None, :, None])
    ).astype(jnp.float32)
    inside = jnp.einsum("bij,bjf->bif", same_mask, grouped, precision=lax.Precision.HIGHEST)
    inside_count = jnp.sum(same_mask, axis=2)
    first_ids = grouped_ids[:, 0]
    row_index = jnp.arange(rows_dev)
    block_start = jnp.arange(block_count) * block_rows
    earlier_rows = (
        (session[None, :] == first_ids[:, None]) & (row_index[None, :] < block_start[:, None])
    ).astype(jnp.float32)
    carried = jnp.dot(earlier_rows, features, precision=lax.Precision.HIGHEST)
    carried_count = jnp.sum(earlier_rows, axis=1)
    joined = grouped_ids == first_ids[:, None]
    partial_rows = inside + jnp.where(joined[:, :, None], carried[:, None, :], 0.0)
    partial_count = inside_count + jnp.where(joined, carried_count[:, None], 0.0)
    return (partial_rows.reshape(rows_dev, feature_width), partial_count.reshape(rows_dev))


def chain_join(earlier, latter):
    early_meta, early_tail = earlier
    late_meta, late_tail = latter
    first_id = jnp.where(early_meta[0] < 0, late_meta[0], early_meta[0])
    last_id = jnp.where(late_meta[1] < 0, early_meta[1], late_meta[1])
    joined = (late_meta[0] < 0) | (late_meta[0] == late_meta[1]) & (early_meta[1] == late_meta[0])
    count_rows = late_meta[2] + jnp.where(joined, early_meta[2], 0.0)
    tail_sum = late_tail + jnp.where(joined, early_tail, 0.0)
    return (jnp.stack([first_id, last_id, count_rows]), tail_sum)


def body(features, session, owner_map):
    rows_dev, feature_width = features.shape
    owners = owner_map[0]
    block_count = owners.shape[0]
    block_rows = rows_dev // block_count
    row_count = lax.axis_size("row")
    slot_cap = max(1, 2 * block_count // row_count)
    partial_rows, partial_count = local_sums(features, session, block_count)
    session_float = session.astype(jnp.float32)
    tail_sum = partial_rows[-1]
    tail_count = partial_count[-1]
    own_meta = jnp.stack([session_float[0], session_float[-1], tail_count])
    identity = (jnp.array([-1.0, -1.0, 0.0], jnp.float32), jnp.zeros((feature_width,), jnp.float32))
    carry_meta, carry_tail = prefix((own_meta, tail_sum), ("row", "grp"), chain_join, identity)
    order = jnp.arange(block_count)
    rank = jnp.sum(
        ((owners[:, None] == owners[None, :]) & (order[None, :] < order[:, None])).astype(
            jnp.int32
        ),
        axis=1,
    )
    target = owners * slot_cap + rank
    slot_index = jnp.arange(row_count * slot_cap)
    hit = slot_index[:, None] == target[None, :]
    filled = jnp.any(hit, axis=1)
    source = jnp.sum(jnp.where(hit, order[None, :], 0), axis=1)
    joined = session_float == carry_meta[1]
    total = partial_rows + jnp.where(joined[:, None], carry_tail[None, :], 0.0)
    counted = partial_count + jnp.where(joined, carry_meta[2], 0.0)
    normalized = (total / jnp.sqrt(counted)[:, None]).astype(jnp.bfloat16)
    normalized = normalized.reshape(block_count, block_rows, feature_width)
    outgoing = jnp.where(filled[:, None, None], normalized[source], jnp.zeros((), jnp.bfloat16))
    return lax.all_to_all(outgoing, "row", split_axis=0, concat_axis=0, tiled=True)


def solution(mesh):
    in_specs = (P(("row", "grp"), None), P(("row", "grp")), P(("row", "grp"), None))
    out_specs = P(("row", "grp"), None, None)
    return jax.shard_map(body, mesh=mesh, in_specs=in_specs, out_specs=out_specs, check_vma=False)
```

profile of v0, /device:TPU:0, one launch (start us, length us, event | category | flops | bytes accessed | tf_op | source)
XLA Modules:
  0.0 519.4 jit_solution(1333118981943403460)
XLA Ops:
  0.0 0.9 convert_reduce_fusion.2
  0.9 0.7 fusion.12
  1.8 0.7 convert_element_type.17
  2.5 0.8 eq.103
  4.1 1.1 convert_reduce_fusion.1
  5.5 1.3 convert_reduce_fusion
  6.9 0.7 select_add_fusion.1
  8.2 2.1 maximum_dynamic-update-slice_fusion
  10.2 41.9 %all-reduce = f32[96]{0:T(128)S(1)} all-reduce(f32[96]{0:T(128)S(1)} %maximum_dynamic-update-slice_fusion), channel_id=2, replica_groups=mesh['row'=16,'grp'=2] {'row','grp'}, use_global_device_ids=true, to_apply=%add | all-reduce | flops 96 | bytes 768
  52.3 4.2 fusion.4
  56.6 3.1 select_add_fusion
  59.7 2.0 copy-done
  61.7 40.2 %all-gather.1 = f32[32,1,256]{2,1,0:T(1,128)S(1)} all-gather(f32[1,1,256]{2,1,0:T(1,128)S(1)} %slice_bitcast_fusion), channel_id=1, replica_groups=mesh['row'=16,'grp'=2] {'row','grp'}, dimensions={0}, use_global_device_ids=true | all-gather | bytes 33792 | tf_op jit(solution)/shard_map/all_gather | solution.py:9
  101.9 307.6 %while.16 = (s32[]{:T(128)}, f32[3]{0:T(128)S(1)}, f32[256]{0:T(256)S(1)}, s32[]{:T(128)}, f32[32,3]{1,0:T(8,128)S(1)}, /*index=5*/f32[32,256]{1,0:T(8,128)S(1)}, s32[]{:T(128)}, f32[]{:T(128)}, s32[]{:T(128)}) while((s32[]{:T(128)}, f32[3]{0:T(128)S(1)}, f32[256]{0:T(256)S(1)}, s32[]{:T(128)}, f32[32,3]{1,0:T(8,128)S(1)}, ...), condition=%wide.region_5.6_spmd.clone, body=%wide.region_4.5_spmd.clone.sunk | while | flops 1048 | bytes 5461 | solution.py:21
  105.1 0.7 fusion.22
  114.7 0.7 fusion.22
  124.3 0.7 fusion.22
  134.0 0.7 fusion.22
  143.6 0.7 fusion.22
  153.2 0.7 fusion.22
  162.8 0.7 fusion.22
  172.4 0.7 fusion.22
  182.0 0.7 fusion.22
  191.6 0.7 fusion.22
  201.3 0.7 fusion.22
  210.9 0.7 fusion.22
  220.5 0.7 fusion.22
  230.1 0.7 fusion.22
  239.7 0.7 fusion.22
  249.3 0.7 fusion.22
  258.9 0.7 fusion.22
  268.5 0.7 fusion.22
  278.2 0.7 fusion.22
  287.8 0.7 fusion.22
  297.4 0.7 fusion.22
  307.0 0.7 fusion.22
  316.6 0.7 fusion.22
  326.2 0.7 fusion.22
  335.8 0.7 fusion.22
  345.4 0.7 fusion.22
  355.1 0.7 fusion.22
  374.3 0.7 fusion.22
  410.2 1.3 add_sqrt_fusion
  411.6 3.6 divide_convert_fusion
  415.2 2.8 gather_fusion
  418.0 2.5 broadcast_select_fusion.1
  420.6 96.8 %all_to_all.5 = bf16[128,64,256]{2,1,0:T(8,128)(2,1)S(1)} all-to-all(bf16[128,64,256]{2,1,0:T(8,128)(2,1)S(1)} %broadcast_select_fusion.1), channel_id=1, replica_groups=mesh['row'=16,'grp'=2] {'row'}, dimensions={0} | all-to-all | bytes 8388608 | tf_op jit(solution)/shard_map/all_to_all | solution.py:93
  517.4 2.0 copy.33
  (194 shorter events, 28.9 us)
Async XLA Ops:
  52.3 4.3 copy-start.1
  56.5 45.4 %copy-start.3 = (f32[3]{0:T(128)S(1)}, f32[3]{0:T(128)}, u32[]{:S(2)}) copy-start(f32[3]{0:T(128)} %constant.55.clone) | copy-start | bytes 40
  56.5 353.6 %copy-start.2 = (s32[4096]{0:T(1024)S(1)}, s32[4096]{0:T(1024)}, u32[]{:S(2)}) copy-start(s32[4096]{0:T(1024)} %param.7) | copy-start | bytes 49156
  59.7 2.0 copy-start
where the time goes:
time: 524 us; the launch traced here: 519 us
  loops' own time  263 us (50%)
  blocking collectives  179 us (34%)
  local copies, waits for them, and re-layouts  51.8 us (10%)
  other arithmetic  18.2 us (3%)
  matrix products  7.35 us (1%)
    another operation x1, loops' own time, prefix(): return lax.fori_loop(0, size, turn, start)  263 us
    all_to_all x1, blocking collectives, body(): lax.all_to_all(outgoing, 'row', split_axis=0, concat_axis=0, tiled=True)  96.8 us
    unnamed x1, blocking collectives  41.9 us
    all_gather x1, blocking collectives, prefix(): everything = jax.tree.map(lambda part: lax.all_gather(part, axis), array)  40.2 us
    slice x32, local copies, waits for them, and re-layouts, chain_join(): first_id = jnp.where(early_meta[0] < 0, late_meta[0], early_meta[0])  21.3 us
    slice x32, local copies, waits for them, and re-layouts, chain_join(): last_id = jnp.where(late_meta[1] < 0, early_meta[1], late_meta[1])  19.5 us

commit v1 on v0

v1 whole, which is shorter than its diff:
```python
import functools

import jax
import jax.numpy as jnp
from jax import lax
from jax.experimental import pallas as pl
from jax.experimental.pallas import tpu as pltpu
from jax.sharding import PartitionSpec as P

LANES = 128
AXES = ("row", "grp")


def tail_kernel(ids_ref, x_ref, out_ref, acc_ref, *, rows):
    step = pl.program_id(0)
    chunk, width = x_ref.shape
    ids = ids_ref[...]
    id_rows = ids.shape[0]
    last = ids_ref[id_rows - 1 : id_rows, LANES - 1 : LANES]
    in_tail = jnp.where(ids == last, 1, 0)
    count = jnp.sum(jnp.sum(in_tail, axis=0, keepdims=True), axis=1, keepdims=True)

    @pl.when(step == 0)
    def _():
        acc_ref[...] = jnp.zeros_like(acc_ref)

    row = lax.broadcasted_iota(jnp.int32, (chunk, width), 0) + step * chunk
    kept = jnp.where(row >= rows - count, x_ref[...], 0.0)
    acc_ref[...] += jnp.sum(kept.reshape(chunk // 8, 8, width), axis=0)

    @pl.when(step == pl.num_programs(0) - 1)
    def _():
        copies = out_ref.shape[0]
        tail = jnp.sum(acc_ref[...], axis=0, keepdims=True)
        out_ref[:, :width] = jnp.broadcast_to(tail, (copies, width))
        lane = lax.broadcasted_iota(jnp.int32, (copies, LANES), 1)
        first = ids_ref[0:1, 0:1]
        meta = jnp.where(lane == 0, first, jnp.where(lane == 1, last, count))
        out_ref[:, width:] = meta.astype(jnp.float32)


def tails(ids, features, copies):
    rows, width = features.shape
    chunk = rows // 8
    return pl.pallas_call(
        functools.partial(tail_kernel, rows=rows),
        grid=(rows // chunk,),
        in_specs=[
            pl.BlockSpec(ids.shape, lambda i: (0, 0)),
            pl.BlockSpec((chunk, width), lambda i: (i, 0)),
        ],
        out_specs=pl.BlockSpec((copies, width + LANES), lambda i: (0, 0)),
        out_shape=jax.ShapeDtypeStruct((copies, width + LANES), jnp.float32),
        scratch_shapes=[pltpu.VMEM((8, width), jnp.float32)],
        name="tails",
    )(ids, features)


def blocks_kernel(
    here_ref, owners_ref, ids_ref, all_ref, x_ref, out_ref,
    norm_ref, zero_ref, sum_ref, count_ref, slot_ref, used_ref, sem, *, cap
):
    step = pl.program_id(0)
    chunk, width = x_ref.shape
    blocks, block_rows, _ = norm_ref.shape
    owners = out_ref.shape[0] // cap
    tile = LANES
    tiles = chunk // tile
    ids_rows = ids_ref.shape[0]

    @pl.when(step == 0)
    def _():
        zero_ref[...] = jnp.zeros_like(zero_ref)
        first = ids_ref[0:1, 0:1].astype(jnp.float32)
        device = lax.broadcasted_iota(jnp.int32, (all_ref.shape[0], 1), 0)
        feeds = (device < here_ref[0]) & (all_ref[:, width + 1 : width + 2] == first)
        sum_ref[...] = jnp.sum(jnp.where(feeds, all_ref[:, :width], 0.0), axis=0, keepdims=True)
        counts = jnp.where(feeds, all_ref[:, width + 2 : width + 3], 0.0)
        count_ref[...] = jnp.broadcast_to(jnp.sum(counts, axis=0, keepdims=True), count_ref.shape)

        @pl.loop(0, owners)
        def _(o):
            used_ref[o] = 0

        @pl.loop(0, blocks)
        def _(b):
            o = owners_ref[0, b]
            rank = used_ref[o]
            used_ref[o] = rank + 1
            slot_ref[b] = o * cap + rank

        @pl.loop(0, owners)
        def _(o):
            @pl.loop(used_ref[o], cap)
            def _(k):
                pltpu.make_async_copy(zero_ref, out_ref.at[o * cap + k], sem).start()

    lower = lax.broadcasted_iota(jnp.int32, (tile, tile), 1) <= lax.broadcasted_iota(
        jnp.int32, (tile, tile), 0
    )
    ones = jnp.ones((tile, LANES), jnp.bfloat16)
    row = lax.broadcasted_iota(jnp.int32, (tile, LANES), 0)
    carry = sum_ref[...]
    carry_count = count_ref[...]
    for k in range(tiles):
        t = step * tiles + k
        id_row = ids_ref[pl.ds(t, 1), :].astype(jnp.float32)
        before = ids_ref[pl.ds(jnp.maximum(t - 1, 0), 1), LANES - 1 : LANES].astype(jnp.float32)
        if k == 0:
            before = jnp.where(t == 0, id_row[:, :1], before)
        ids = jnp.broadcast_to(id_row, (tile, tile))
        same = (ids == ids.T) & lower
        mask = jnp.where(same, 1.0, 0.0).astype(jnp.bfloat16)
        x = x_ref[pl.ds(k * tile, tile), :]
        high = x.astype(jnp.bfloat16)
        rest = x - high.astype(jnp.float32)
        middle = rest.astype(jnp.bfloat16)
        low = (rest - middle.astype(jnp.float32)).astype(jnp.bfloat16)
        total = (
            jnp.dot(mask, low, preferred_element_type=jnp.float32)
            + jnp.dot(mask, middle, preferred_element_type=jnp.float32)
        ) + jnp.dot(mask, high, preferred_element_type=jnp.float32)
        count = jnp.dot(mask, ones, preferred_element_type=jnp.float32)
        joined = jnp.sum(jnp.where(id_row == before, 1, 0), axis=1, keepdims=True)
        follows = row < joined
        follows_wide = jnp.concatenate([follows] * (width // LANES), axis=1)
        total = total + jnp.where(follows_wide, carry, 0.0)
        count = count + jnp.where(follows, carry_count, 0.0)
        carry = total[tile - 1 :, :]
        carry_count = count[tile - 1 :, :]
        scale = lax.rsqrt(count)
        value = (total * jnp.concatenate([scale] * (width // LANES), axis=1)).astype(jnp.bfloat16)
        per_tile = tile // block_rows
        for p in range(per_tile):
            b = t * per_tile + p
            norm_ref[b] = value[p * block_rows : (p + 1) * block_rows, :]
            pltpu.make_async_copy(norm_ref.at[b], out_ref.at[slot_ref[b]], sem).start()
    sum_ref[...] = carry
    count_ref[...] = carry_count

    @pl.when(step == pl.num_programs(0) - 1)
    def _():
        pltpu.make_async_copy(out_ref, out_ref, sem).wait()


def slotted(here, owners, ids, everything, features, slots, cap):
    rows, width = features.shape
    blocks = owners.shape[1]
    block_rows = rows // blocks
    chunk = rows // 8
    return pl.pallas_call(
        functools.partial(blocks_kernel, cap=cap),
        grid=(rows // chunk,),
        in_specs=[
            pl.BlockSpec(memory_space=pltpu.SMEM),
            pl.BlockSpec(memory_space=pltpu.SMEM),
            pl.BlockSpec(ids.shape, lambda i: (0, 0)),
            pl.BlockSpec(everything.shape, lambda i: (0, 0)),
            pl.BlockSpec((chunk, width), lambda i: (i, 0)),
        ],
        out_specs=pl.BlockSpec(memory_space=pl.ANY),
        out_shape=jax.ShapeDtypeStruct((slots, block_rows, width), jnp.bfloat16),
        scratch_shapes=[
            pltpu.VMEM((blocks, block_rows, width), jnp.bfloat16),
            pltpu.VMEM((block_rows, width), jnp.bfloat16),
            pltpu.VMEM((1, width), jnp.float32),
            pltpu.VMEM((1, LANES), jnp.float32),
            pltpu.SMEM((blocks,), jnp.int32),
            pltpu.SMEM((slots // cap,), jnp.int32),
            pltpu.SemaphoreType.DMA,
        ],
        name="slotted",
    )(here, owners, ids, everything, features)


def body(features, session, owner_map):
    rows, _ = features.shape
    blocks = owner_map.shape[1]
    row_count, grp_count = lax.axis_size("row"), lax.axis_size("grp")
    cap = max(1, 2 * blocks // row_count)
    ids = session.reshape(rows // LANES, LANES)
    everything = lax.all_to_all(
        tails(ids, features, row_count * grp_count), AXES, split_axis=0, concat_axis=0, tiled=True
    )
    here = (lax.axis_index("row") * grp_count + lax.axis_index("grp")).reshape(1)
    outgoing = slotted(here, owner_map, ids, everything, features, row_count * cap, cap)
    return lax.all_to_all(outgoing, "row", split_axis=0, concat_axis=0, tiled=True)


def solution(mesh):
    in_specs = (P(AXES, None), P(AXES), P(AXES, None))
    return jax.shard_map(
        body, mesh=mesh, in_specs=in_specs, out_specs=P(AXES, None, None), check_vma=False
    )
```

time: 524 us -> 132 us (0.25)
  loops' own time: 263 us -> 0 us
  blocking collectives: 179 us -> 97.8 us
  local copies, waits for them, and re-layouts: 51.8 us -> 4.09 us
  other arithmetic: 18.2 us -> 0 us
  Pallas kernels: 0 us -> 15.2 us
  matrix products: 7.35 us -> 0 us
  starting transfers between devices: 0 us -> 7.33 us
  waiting for transfers between devices: 0 us -> 7.33 us
    another operation x1 -> x0, loops' own time: 263 us -> none  [prefix(): return lax.fori_loop(0, size, turn, start)]
    slice x68 -> x0, local copies, waits for them, and re-layouts: 42.8 us -> none  [the longest x32 21.3 us: chain_join(): first_id = jnp.where(early_meta[0] < 0, late_meta[0], early_meta[0])]
    unnamed x1 -> x0, blocking collectives: 41.9 us -> none
    all_gather x1 -> x0, blocking collectives: 40.2 us -> none  [prefix(): everything = jax.tree.map(lambda part: lax.all_gather(part, axis), array)]
    pallas_call x0 -> x2, Pallas kernels: none -> 15.2 us  [the longest x1 8.85 us: slotted(): pl.pallas_call(functools.partial(blocks_kernel, cap=cap), grid=(rows // c...]
    dot_general x2 -> x0, matrix products: 7.35 us -> none  [the longest x1 4.24 us: local_sums(): carried = jnp.dot(earlier_rows, features, precision=lax.Precision.HIGHEST)]
    all_to_all x0 -> x1, waiting for transfers between devices: none -> 7.33 us  [body(): lax.all_to_all(tails(ids, features, row_count * grp_count), AXES, split_a...]
    all_to_all x0 -> x1, starting transfers between devices: none -> 7.33 us  [body(): lax.all_to_all(tails(ids, features, row_count * grp_count), AXES, split_a...]
  transfers between devices with their start and end apart: 0 -> 1, of which waited for: 0 -> 1; matrix products, arithmetic and copies ran while one was open for 0% -> 0% of each run, Pallas kernels for 0% -> 0%
where the time goes in v1:
time: 132 us
  blocking collectives  97.8 us (74%)
  Pallas kernels  15.2 us (12%)
  starting transfers between devices  7.33 us (6%)
  waiting for transfers between devices  7.33 us (6%)
  local copies, waits for them, and re-layouts  4.09 us (3%)
    all_to_all x1, blocking collectives, body(): lax.all_to_all(outgoing, 'row', split_axis=0, concat_axis=0, tiled=True)  97.8 us
    pallas_call x1, Pallas kernels, slotted(): pl.pallas_call(functools.partial(blocks_kernel, cap=cap), grid=(rows // c...  8.85 us
    all_to_all x1, waiting for transfers between devices, body(): lax.all_to_all(tails(ids, features, row_count * grp_count), AXES, split_a...  7.33 us
    all_to_all x1, starting transfers between devices, body(): lax.all_to_all(tails(ids, features, row_count * grp_count), AXES, split_a...  7.33 us
    pallas_call x1, Pallas kernels, tails(): pl.pallas_call(functools.partial(tail_kernel, rows=rows), grid=(rows // c...  6.36 us
  transfers between devices with their start and end apart: 1, of which 1 were waited for; matrix products, arithmetic and copies ran while one was open for 0% of the time, Pallas kernels for 0%

profile of v1, /device:TPU:0, one launch (start us, length us, event | category | flops | bytes accessed | tf_op | source)
XLA Modules:
  0.0 131.8 jit_solution(12569548963516372939)
XLA Ops:
  0.0 6.4 %tails.1 = f32[32,384]{1,0:T(8,128)} custom-call(s32[32,128]{1,0:T(8,128)} %bitcast.8, f32[4096,256]{1,0:T(8,128)} %x_ref.3), custom_call_target="tpu_custom_call" | custom-call | tf_op jit(solution)/shard_map/tails/pallas_call | solution.py:45
  6.4 1.5 %copy.4 = f32[32,1,384]{2,1,0:T(1,128)} copy(f32[32,1,384]{2,0,1:T(8,128)} %bitcast.7) | data formatting | bytes 98304 | tf_op jit(solution)/shard_map/all_to_all | solution.py:182
  7.8 7.3 %all-to-all-start = ((f32[32,1,384]{2,1,0:T(1,128)}), f32[32,1,384]{2,1,0:T(1,128)S(1)}, u32[]{:S(2)}, u32[]{:S(2)}) async-start(f32[32,1,384]{2,1,0:T(1,128)} %copy.4), calls=%async_computation | async-start | bytes 98304 | tf_op jit(solution)/shard_map/all_to_all | solution.py:182
  15.2 7.3 %all-to-all-done = f32[32,1,384]{2,1,0:T(1,128)S(1)} async-done(((f32[32,1,384]{2,1,0:T(1,128)}), f32[32,1,384]{2,1,0:T(1,128)S(1)}, u32[]{:S(2)}, u32[]{:S(2)}) %all-to-all-start) | async-done | bytes 49184 | tf_op jit(solution)/shard_map/all_to_all | solution.py:182
  22.5 0.6 copy.7
  23.1 8.9 %slotted.1 = bf16[128,64,256]{2,1,0:T(8,128)(2,1)} custom-call(s32[1]{0:T(128)} %bitcast.here_ref, s32[1,64]{1,0:T(1,128)} %owners_ref.1, s32[32,128]{1,0:T(8,128)} %bitcast.9, f32[32,384]{1,0:T(8,128)} %bitcast.6, f32[4096,256]{1,0:T(8,128)} %x_ref.3), custom_call_target="tpu_custom_call" | custom-call | tf_op jit(solution)/shard_map/slotted/pallas_call | solution.py:151
  32.0 97.8 %all_to_all.16 = bf16[128,64,256]{2,1,0:T(8,128)(2,1)S(1)} all-to-all(bf16[128,64,256]{2,1,0:T(8,128)(2,1)} %slotted.1), channel_id=1, replica_groups=mesh['row'=16,'grp'=2] {'row'}, dimensions={0} | all-to-all | bytes 8388608 | tf_op jit(solution)/shard_map/all_to_all | solution.py:187
  129.8 2.0 %copy.9 = bf16[128,64,256]{2,1,0:T(8,128)(2,1)} copy(bf16[128,64,256]{2,1,0:T(8,128)(2,1)S(1)} %all_to_all.16) | data formatting | bytes 8388608
Async XLA Ops:
  7.8 14.7 %all-to-all-start = ((f32[32,1,384]{2,1,0:T(1,128)}), f32[32,1,384]{2,1,0:T(1,128)S(1)}, u32[]{:S(2)}, u32[]{:S(2)}) async-start(f32[32,1,384]{2,1,0:T(1,128)} %copy.4), calls=%async_computation | async-start | bytes 98304 | tf_op jit(solution)/shard_map/all_to_all | solution.py:182

commit v2 on v1

v2 whole, which is shorter than its diff:
```python
import functools

import jax
import jax.numpy as jnp
from jax import lax
from jax.experimental import pallas as pl
from jax.experimental.pallas import tpu as pltpu
from jax.sharding import PartitionSpec as P

LANES = 128
AXES = ("row", "grp")
PIECES = 8


def piece_copy(hbm_ref, vmem_ref, sem_ref, piece):
    rows = hbm_ref.shape[0] // PIECES
    part = pl.ds(pl.multiple_of(piece * rows, rows), rows)
    return pltpu.make_async_copy(hbm_ref.at[part], vmem_ref.at[part], sem_ref.at[piece])


def tail_kernel(ids_ref, x_hbm, out_ref, x_ref, sem_ref):
    rows, width = x_ref.shape
    chunk = rows // PIECES
    for piece in range(PIECES):
        piece_copy(x_hbm, x_ref, sem_ref, piece).start()
    ids = ids_ref[...]
    id_rows = ids.shape[0]
    last = ids_ref[id_rows - 1 : id_rows, LANES - 1 : LANES]
    in_tail = jnp.where(ids == last, 1, 0)
    count = jnp.sum(jnp.sum(in_tail, axis=0, keepdims=True), axis=1, keepdims=True)
    copies = out_ref.shape[0]
    lane = lax.broadcasted_iota(jnp.int32, (1, LANES), 1)
    meta = jnp.where(lane == 0, ids_ref[0:1, 0:1], jnp.where(lane == 1, last, count))
    row = lax.broadcasted_iota(jnp.int32, (chunk, width), 0)

    def add(piece, total):
        piece_copy(x_hbm, x_ref, sem_ref, piece).wait()
        part = x_ref[pl.ds(pl.multiple_of(piece * chunk, chunk), chunk), :]
        kept = jnp.where(row >= rows - count - piece * chunk, part, 0.0)
        return total + jnp.sum(kept.reshape(chunk // 8, 8, width), axis=0)

    total = lax.fori_loop(0, PIECES, add, jnp.zeros((8, width), jnp.float32))
    tail = jnp.sum(total, axis=0, keepdims=True)
    message = jnp.concatenate([tail, meta.astype(jnp.float32)], axis=1)
    out_ref[...] = jnp.broadcast_to(message[None], out_ref.shape)


def tails(ids, features, copies):
    rows, width = features.shape
    return pl.pallas_call(
        tail_kernel,
        in_specs=[
            pl.BlockSpec(memory_space=pltpu.VMEM),
            pl.BlockSpec(memory_space=pl.ANY),
        ],
        out_specs=pl.BlockSpec(memory_space=pltpu.VMEM),
        out_shape=jax.ShapeDtypeStruct((copies, 1, width + LANES), jnp.float32),
        scratch_shapes=[
            pltpu.VMEM((rows, width), jnp.float32),
            pltpu.SemaphoreType.DMA((PIECES,)),
        ],
        name="tails",
    )(ids, features)


def blocks_kernel(
    here_ref, owners_ref, ids_ref, all_ref, x_hbm, out_ref,
    x_ref, norm_ref, zero_ref, slot_ref, used_ref, sem_ref, sem, *, cap
):
    rows, width = x_ref.shape
    blocks, block_rows, _ = norm_ref.shape
    owners = out_ref.shape[0] // cap
    tile = LANES
    chunk = rows // PIECES
    tiles = chunk // tile
    for piece in range(PIECES):
        piece_copy(x_hbm, x_ref, sem_ref, piece).start()
    zero_ref[...] = jnp.zeros_like(zero_ref)

    @pl.loop(0, owners)
    def _(o):
        used_ref[o] = 0

    @pl.loop(0, blocks)
    def _(b):
        o = owners_ref[0, b]
        rank = used_ref[o]
        used_ref[o] = rank + 1
        slot_ref[b] = o * cap + rank

    @pl.loop(0, owners)
    def _(o):
        @pl.loop(used_ref[o], cap)
        def _(k):
            pltpu.make_async_copy(zero_ref, out_ref.at[o * cap + k], sem).start()

    everything = all_ref[:, 0, :]
    first = ids_ref[0:1, 0:1].astype(jnp.float32)
    device = lax.broadcasted_iota(jnp.int32, (everything.shape[0], 1), 0)
    feeds = (device < here_ref[0]) & (everything[:, width + 1 : width + 2] == first)
    carry = jnp.sum(jnp.where(feeds, everything[:, :width], 0.0), axis=0, keepdims=True)
    carry_count = jnp.sum(
        jnp.where(feeds, everything[:, width + 2 : width + 3], 0.0), axis=0, keepdims=True
    )
    carry_count = jnp.broadcast_to(carry_count, (1, LANES))

    lower = lax.broadcasted_iota(jnp.int32, (tile, tile), 1) <= lax.broadcasted_iota(
        jnp.int32, (tile, tile), 0
    )
    ones = jnp.ones((tile, LANES), jnp.bfloat16)
    row = lax.broadcasted_iota(jnp.int32, (tile, LANES), 0)

    def run(piece, carried):
        carry, carry_count, before = carried
        piece_copy(x_hbm, x_ref, sem_ref, piece).wait()
        for k in range(tiles):
            t = piece * tiles + k
            id_row = ids_ref[pl.ds(t, 1), :].astype(jnp.float32)
            ids = jnp.broadcast_to(id_row, (tile, tile))
            same = (ids == ids.T) & lower
            mask = jnp.where(same, 1.0, 0.0).astype(jnp.bfloat16)
            x = x_ref[pl.ds(pl.multiple_of(t * tile, tile), tile), :]
            high = x.astype(jnp.bfloat16)
            rest = x - high.astype(jnp.float32)
            middle = rest.astype(jnp.bfloat16)
            low = (rest - middle.astype(jnp.float32)).astype(jnp.bfloat16)
            total = (
                jnp.dot(mask, low, preferred_element_type=jnp.float32)
                + jnp.dot(mask, middle, preferred_element_type=jnp.float32)
            ) + jnp.dot(mask, high, preferred_element_type=jnp.float32)
            count = jnp.dot(mask, ones, preferred_element_type=jnp.float32)
            joined = jnp.sum(jnp.where(id_row == before, 1, 0), axis=1, keepdims=True)
            follows = row < joined
            follows_wide = jnp.concatenate([follows] * (width // LANES), axis=1)
            total = total + jnp.where(follows_wide, carry, 0.0)
            count = count + jnp.where(follows, carry_count, 0.0)
            carry = total[tile - 1 :, :]
            carry_count = count[tile - 1 :, :]
            before = id_row[:, LANES - 1 :]
            scale = lax.rsqrt(count)
            value = (total * jnp.concatenate([scale] * (width // LANES), axis=1)).astype(jnp.bfloat16)
            per_tile = tile // block_rows
            for p in range(per_tile):
                b = t * per_tile + p
                norm_ref[b] = value[p * block_rows : (p + 1) * block_rows, :]
                pltpu.make_async_copy(norm_ref.at[b], out_ref.at[slot_ref[b]], sem).start()
        return carry, carry_count, before

    lax.fori_loop(0, PIECES, run, (carry, carry_count, first))
    pltpu.make_async_copy(out_ref, out_ref, sem).wait()


def slotted(here, owners, ids, everything, features, slots, cap):
    rows, width = features.shape
    blocks = owners.shape[1]
    block_rows = rows // blocks
    return pl.pallas_call(
        functools.partial(blocks_kernel, cap=cap),
        in_specs=[
            pl.BlockSpec(memory_space=pltpu.SMEM),
            pl.BlockSpec(memory_space=pltpu.SMEM),
            pl.BlockSpec(memory_space=pltpu.VMEM),
            pl.BlockSpec(memory_space=pltpu.VMEM),
            pl.BlockSpec(memory_space=pl.ANY),
        ],
        out_specs=pl.BlockSpec(memory_space=pl.ANY),
        out_shape=jax.ShapeDtypeStruct((slots, block_rows, width), jnp.bfloat16),
        scratch_shapes=[
            pltpu.VMEM((rows, width), jnp.float32),
            pltpu.VMEM((blocks, block_rows, width), jnp.bfloat16),
            pltpu.VMEM((block_rows, width), jnp.bfloat16),
            pltpu.SMEM((blocks,), jnp.int32),
            pltpu.SMEM((slots // cap,), jnp.int32),
            pltpu.SemaphoreType.DMA((PIECES,)),
            pltpu.SemaphoreType.DMA,
        ],
        name="slotted",
    )(here, owners, ids, everything, features)


def body(features, session, owner_map):
    rows, _ = features.shape
    blocks = owner_map.shape[1]
    row_count, grp_count = lax.axis_size("row"), lax.axis_size("grp")
    cap = max(1, 2 * blocks // row_count)
    ids = session.reshape(rows // LANES, LANES)
    everything = lax.all_to_all(
        tails(ids, features, row_count * grp_count), AXES, split_axis=0, concat_axis=0, tiled=True
    )
    here = (lax.axis_index("row") * grp_count + lax.axis_index("grp")).reshape(1)
    outgoing = slotted(here, owner_map, ids, everything, features, row_count * cap, cap)
    return lax.all_to_all(outgoing, "row", split_axis=0, concat_axis=0, tiled=True)


def solution(mesh):
    in_specs = (P(AXES, None), P(AXES), P(AXES, None))
    return jax.shard_map(
        body, mesh=mesh, in_specs=in_specs, out_specs=P(AXES, None, None), check_vma=False
    )
```

time: 132 us -> 126 us (0.955)
  Pallas kernels: 15.2 us -> 10.4 us
  local copies, waits for them, and re-layouts: 4.09 us -> 2.62 us
    pallas_call x2, Pallas kernels: 15.2 us -> 10.4 us  [the longest x1 6.77 us: slotted(): pl.pallas_call(functools.partial(blocks_kernel, cap=cap), in_specs=[pl.Bl...]
    all_to_all x1 -> x0, local copies, waits for them, and re-layouts: 1.46 us -> none  [body(): lax.all_to_all(tails(ids, features, row_count * grp_count), AXES, split_a...]
where the time goes in v2:
time: 126 us
  blocking collectives  97.8 us (78%)
  Pallas kernels  10.4 us (8%)
  starting transfers between devices  7.33 us (6%)
  waiting for transfers between devices  7.33 us (6%)
  local copies, waits for them, and re-layouts  2.62 us (2%)
    all_to_all x1, blocking collectives, body(): lax.all_to_all(outgoing, 'row', split_axis=0, concat_axis=0, tiled=True)  97.8 us
    all_to_all x1, starting transfers between devices, body(): lax.all_to_all(tails(ids, features, row_count * grp_count), AXES, split_a...  7.33 us
    all_to_all x1, waiting for transfers between devices, body(): lax.all_to_all(tails(ids, features, row_count * grp_count), AXES, split_a...  7.33 us
    pallas_call x1, Pallas kernels, slotted(): pl.pallas_call(functools.partial(blocks_kernel, cap=cap), in_specs=[pl.Bl...  6.77 us
    pallas_call x1, Pallas kernels, tails(): pl.pallas_call(tail_kernel, in_specs=[pl.BlockSpec(memory_space=pltpu.VME...  3.67 us
    unnamed x3, local copies, waits for them, and re-layouts  2.62 us
  transfers between devices with their start and end apart: 1, of which 1 were waited for; matrix products, arithmetic and copies ran while one was open for 0% of the time, Pallas kernels for 0%

profile of v2, /device:TPU:0, one launch (start us, length us, event | category | flops | bytes accessed | tf_op | source)
XLA Modules:
  0.0 125.6 jit_solution(2009349850785770983)
XLA Ops:
  0.0 3.7 %tails.1 = f32[32,1,384]{2,1,0:T(1,128)} custom-call(s32[32,128]{1,0:T(8,128)} %bitcast.2, f32[4096,256]{1,0:T(8,128)} %x_hbm.3), custom_call_target="tpu_custom_call" | custom-call | tf_op jit(solution)/shard_map/tails/pallas_call | solution.py:50
  3.7 7.3 %all-to-all-start = ((f32[32,1,384]{2,1,0:T(1,128)}), f32[32,1,384]{2,1,0:T(1,128)S(1)}, u32[]{:S(2)}, u32[]{:S(2)}) async-start(f32[32,1,384]{2,1,0:T(1,128)} %tails.1), calls=%async_computation | async-start | bytes 98304 | tf_op jit(solution)/shard_map/all_to_all | solution.py:187
  11.0 7.3 %all-to-all-done.all_ref = f32[32,1,384]{2,1,0:T(1,128)S(1)} async-done(((f32[32,1,384]{2,1,0:T(1,128)}), f32[32,1,384]{2,1,0:T(1,128)S(1)}, u32[]{:S(2)}, u32[]{:S(2)}) %all-to-all-start) | async-done | bytes 49184 | tf_op jit(solution)/shard_map/all_to_all | solution.py:187
  18.3 0.0 copy-start
  18.3 0.6 copy-done
  19.0 6.8 %slotted.1 = bf16[128,64,256]{2,1,0:T(8,128)(2,1)} custom-call(s32[1]{0:T(128)} %bitcast.here_ref, s32[1,64]{1,0:T(1,128)} %owners_ref.1, s32[32,128]{1,0:T(8,128)} %bitcast.3, f32[32,1,384]{2,1,0:T(1,128)} %copy-done, f32[4096,256]{1,0:T(8,128)} %x_hbm.3), custom_call_target="tpu_custom_call" | custom-call | tf_op jit(solution)/shard_map/slotted/pallas_call | solution.py:157
  25.7 97.8 %all_to_all.10 = bf16[128,64,256]{2,1,0:T(8,128)(2,1)S(1)} all-to-all(bf16[128,64,256]{2,1,0:T(8,128)(2,1)} %slotted.1), channel_id=1, replica_groups=mesh['row'=16,'grp'=2] {'row'}, dimensions={0} | all-to-all | bytes 8388608 | tf_op jit(solution)/shard_map/all_to_all | solution.py:192
  123.6 2.0 %copy.5 = bf16[128,64,256]{2,1,0:T(8,128)(2,1)} copy(bf16[128,64,256]{2,1,0:T(8,128)(2,1)S(1)} %all_to_all.10) | data formatting | bytes 8388608
Async XLA Ops:
  3.7 14.7 %all-to-all-start = ((f32[32,1,384]{2,1,0:T(1,128)}), f32[32,1,384]{2,1,0:T(1,128)S(1)}, u32[]{:S(2)}, u32[]{:S(2)}) async-start(f32[32,1,384]{2,1,0:T(1,128)} %tails.1), calls=%async_computation | async-start | bytes 98304 | tf_op jit(solution)/shard_map/all_to_all | solution.py:187
  18.3 0.6 copy-start

commit v3 on v2

v3 whole, which is shorter than its diff:
```python
import functools

import jax
import jax.numpy as jnp
from jax import lax
from jax.experimental import pallas as pl
from jax.experimental.pallas import tpu as pltpu
from jax.sharding import PartitionSpec as P


LANES = 128
AXES = ("row", "grp")
PIECES = 8
VMEM = pl.BlockSpec(memory_space=pltpu.VMEM)
SMEM = pl.BlockSpec(memory_space=pltpu.SMEM)
ANY = pl.BlockSpec(memory_space=pl.ANY)
HBM = pl.BlockSpec(memory_space=pltpu.HBM)


def piece_copy(hbm_ref, vmem_ref, sem_ref, piece):
    rows = hbm_ref.shape[0] // PIECES
    part = pl.ds(pl.multiple_of(piece * rows, rows), rows)
    return pltpu.make_async_copy(hbm_ref.at[part], vmem_ref.at[part], sem_ref.at[piece])


def tail_kernel(place_ref, ids_ref, owners_ref, x_hbm, out_ref, x_ref, sem_ref, *, row_count, direct):
    rows, width = x_ref.shape
    chunk = rows // PIECES
    for piece in range(PIECES):
        piece_copy(x_hbm, x_ref, sem_ref, piece).start()
    ids = ids_ref[...]
    id_rows = ids.shape[0]
    last = ids_ref[id_rows - 1 : id_rows, LANES - 1 : LANES]
    in_tail = jnp.where(ids == last, 1, 0)
    count = jnp.sum(jnp.sum(in_tail, axis=0, keepdims=True), axis=1, keepdims=True)
    owners = owners_ref[...]
    blocks = owners.shape[1]
    owner = lax.broadcasted_iota(jnp.int32, (row_count, blocks), 0)
    sent = jnp.sum(jnp.where(owner == owners, 1, 0), axis=1, keepdims=True)
    half = max(1, row_count // 2)
    across = lax.broadcasted_iota(jnp.int32, (row_count, 1), 0) // half != place_ref[1] // half
    packed = jnp.sum(jnp.where(across, jnp.maximum(sent - direct, 0), 0), axis=0, keepdims=True)
    lane = lax.broadcasted_iota(jnp.int32, (1, LANES), 1)
    meta = jnp.where(lane == 2, count, packed)
    meta = jnp.where(lane == 0, ids_ref[0:1, 0:1], jnp.where(lane == 1, last, meta))
    row = lax.broadcasted_iota(jnp.int32, (chunk, width), 0)

    def add(piece, total):
        piece_copy(x_hbm, x_ref, sem_ref, piece).wait()
        part = x_ref[pl.ds(pl.multiple_of(piece * chunk, chunk), chunk), :]
        kept = jnp.where(row >= rows - count - piece * chunk, part, 0.0)
        return total + jnp.sum(kept.reshape(chunk // 8, 8, width), axis=0)

    total = lax.fori_loop(0, PIECES, add, jnp.zeros((8, width), jnp.float32))
    tail = jnp.sum(total, axis=0, keepdims=True)
    room = out_ref.shape[2] - width - LANES
    message = jnp.concatenate(
        [tail, meta.astype(jnp.float32), jnp.zeros((1, room), jnp.float32)], axis=1
    )
    out_ref[...] = jnp.broadcast_to(message[None], out_ref.shape)
    out_ref[:, :, width + LANES : width + LANES + blocks] = jnp.broadcast_to(
        owners.astype(jnp.float32)[None], (out_ref.shape[0], 1, blocks)
    )


def tails(place, ids, owners, features, copies, row_count, direct):
    rows, width = features.shape
    room = pl.cdiv(owners.shape[1], LANES) * LANES
    return pl.pallas_call(
        functools.partial(tail_kernel, row_count=row_count, direct=direct),
        in_specs=[SMEM, VMEM, VMEM, ANY],
        out_specs=VMEM,
        out_shape=jax.ShapeDtypeStruct((copies, 1, width + LANES + room), jnp.float32),
        scratch_shapes=[
            pltpu.VMEM((rows, width), jnp.float32),
            pltpu.SemaphoreType.DMA((PIECES,)),
        ],
        name="tails",
    )(place, ids, owners, features)


def place_blocks(owners_ref, used_ref, blocks, owner_count, put):
    @pl.loop(0, owner_count)
    def _(o):
        used_ref[o] = 0

    def one(b, packed):
        o = owners_ref[0, b]
        rank = used_ref[o]
        used_ref[o] = rank + 1
        return put(b, o, rank, packed)

    return lax.fori_loop(0, blocks, one, 0)


def blocks_kernel(
    place_ref, owners_ref, ids_ref, all_ref, x_hbm, *refs, owner_count, cap, direct, half
):
    outs, (x_ref, norm_ref, zero_ref, slot_ref, used_ref, sem_ref, done_ref) = refs[:-7], refs[-7:]
    rows, width = x_ref.shape
    blocks, block_rows, _ = norm_ref.shape
    tile = LANES
    chunk = rows // PIECES
    tiles = chunk // tile
    for piece in range(PIECES):
        piece_copy(x_hbm, x_ref, sem_ref, piece).start()
    zero_ref[...] = jnp.zeros_like(zero_ref)
    firsts = [0, half * cap, half * (cap + direct)]
    my_half = place_ref[1] // half
    me = place_ref[1] % half

    def put(b, o, rank, packed):
        local = o % half
        near = local * cap + rank
        if half == owner_count:
            slot_ref[b] = near
            return packed
        across = o // half != my_half
        over = across & (rank >= direct)
        far = firsts[1] + (local ^ me) * direct + rank
        slot_ref[b] = jnp.where(over, firsts[2] + packed, jnp.where(across, far, near))
        return packed + jnp.where(over, 1, 0)

    packed = place_blocks(owners_ref, used_ref, blocks, owner_count, put)

    def clear(kind, slot):
        pltpu.make_async_copy(zero_ref, outs[kind].at[slot], done_ref.at[kind]).start()

    @pl.loop(0, half)
    def _(o):
        @pl.loop(used_ref[my_half * half + o], cap)
        def _(k):
            clear(0, o * cap + k)

    if half < owner_count:
        @pl.loop(0, half)
        def _(o):
            @pl.loop(jnp.minimum(used_ref[(1 - my_half) * half + o], direct), direct)
            def _(k):
                clear(1, (o ^ me) * direct + k)

        @pl.loop(packed, outs[2].shape[0])
        def _(k):
            clear(2, k)

    def send(b):
        code = slot_ref[b]
        for kind in range(len(outs)):
            inside = code >= firsts[kind]
            if kind + 1 < len(outs):
                inside = inside & (code < firsts[kind + 1])

            @pl.when(inside)
            def _():
                pltpu.make_async_copy(
                    norm_ref.at[b], outs[kind].at[code - firsts[kind]], done_ref.at[kind]
                ).start()

    everything = all_ref[:, 0, :]
    first = ids_ref[0:1, 0:1].astype(jnp.float32)
    device = lax.broadcasted_iota(jnp.int32, (everything.shape[0], 1), 0)
    feeds = (device < place_ref[0]) & (everything[:, width + 1 : width + 2] == first)
    carry = jnp.sum(jnp.where(feeds, everything[:, :width], 0.0), axis=0, keepdims=True)
    carry_count = jnp.sum(
        jnp.where(feeds, everything[:, width + 2 : width + 3], 0.0), axis=0, keepdims=True
    )
    carry_count = jnp.broadcast_to(carry_count, (1, LANES))

    lower = lax.broadcasted_iota(jnp.int32, (tile, tile), 1) <= lax.broadcasted_iota(
        jnp.int32, (tile, tile), 0
    )
    ones = jnp.ones((tile, LANES), jnp.bfloat16)
    row = lax.broadcasted_iota(jnp.int32, (tile, LANES), 0)

    def run(piece, carried):
        carry, carry_count, before = carried
        piece_copy(x_hbm, x_ref, sem_ref, piece).wait()
        for k in range(tiles):
            t = piece * tiles + k
            id_row = ids_ref[pl.ds(t, 1), :].astype(jnp.float32)
            ids = jnp.broadcast_to(id_row, (tile, tile))
            same = (ids == ids.T) & lower
            mask = jnp.where(same, 1.0, 0.0).astype(jnp.bfloat16)
            x = x_ref[pl.ds(pl.multiple_of(t * tile, tile), tile), :]
            high = x.astype(jnp.bfloat16)
            rest = x - high.astype(jnp.float32)
            middle = rest.astype(jnp.bfloat16)
            low = (rest - middle.astype(jnp.float32)).astype(jnp.bfloat16)
            total = (
                jnp.dot(mask, low, preferred_element_type=jnp.float32)
                + jnp.dot(mask, middle, preferred_element_type=jnp.float32)
            ) + jnp.dot(mask, high, preferred_element_type=jnp.float32)
            count = jnp.dot(mask, ones, preferred_element_type=jnp.float32)
            joined = jnp.sum(jnp.where(id_row == before, 1, 0), axis=1, keepdims=True)
            follows = row < joined
            follows_wide = jnp.concatenate([follows] * (width // LANES), axis=1)
            total = total + jnp.where(follows_wide, carry, 0.0)
            count = count + jnp.where(follows, carry_count, 0.0)
            carry = total[tile - 1 :, :]
            carry_count = count[tile - 1 :, :]
            before = id_row[:, LANES - 1 :]
            scale = lax.rsqrt(count)
            value = (total * jnp.concatenate([scale] * (width // LANES), axis=1)).astype(jnp.bfloat16)
            per_tile = tile // block_rows
            for p in range(per_tile):
                b = t * per_tile + p
                norm_ref[b] = value[p * block_rows : (p + 1) * block_rows, :]
                send(b)
        return carry, carry_count, before

    lax.fori_loop(0, PIECES, run, (carry, carry_count, first))
    for kind, out in enumerate(outs):
        pltpu.make_async_copy(out, out, done_ref.at[kind]).wait()


def slotted(place, owners, ids, everything, features, owner_count, cap, direct, half, size):
    rows, width = features.shape
    blocks = owners.shape[1]
    block_rows = rows // blocks
    counts = [half * cap] + ([half * direct, size] if half < owner_count else [])
    return pl.pallas_call(
        functools.partial(
            blocks_kernel, owner_count=owner_count, cap=cap, direct=direct, half=half
        ),
        in_specs=[SMEM, SMEM, VMEM, VMEM, ANY],
        out_specs=[HBM] * len(counts),
        out_shape=[jax.ShapeDtypeStruct((n, block_rows, width), jnp.bfloat16) for n in counts],
        scratch_shapes=[
            pltpu.VMEM((rows, width), jnp.float32),
            pltpu.VMEM((blocks, block_rows, width), jnp.bfloat16),
            pltpu.VMEM((block_rows, width), jnp.bfloat16),
            pltpu.SMEM((blocks,), jnp.int32),
            pltpu.SMEM((owner_count,), jnp.int32),
            pltpu.SemaphoreType.DMA((PIECES,)),
            pltpu.SemaphoreType.DMA((3,)),
        ],
        name="slotted",
    )(place, owners, ids, everything, features)


def unpack_kernel(
    place_ref, owners_ref, packed_ref, out_ref, zero_ref, from_ref, used_ref, sem,
    *, owner_count, direct, half
):
    blocks = owners_ref.shape[1]
    extra = out_ref.shape[0] // half
    my_half = place_ref[1] // half
    zero_ref[...] = jnp.zeros_like(zero_ref)

    @pl.loop(0, half * extra)
    def _(s):
        from_ref[s] = -1

    def put(b, o, rank, packed):
        here = (rank >= direct) & (o // half == my_half)

        @pl.when(here)
        def _():
            from_ref[(o % half) * extra + rank - direct] = packed

        return packed + jnp.where(here, 1, 0)

    place_blocks(owners_ref, used_ref, blocks, owner_count, put)

    @pl.loop(0, half * extra)
    def _(s):
        source = from_ref[s]

        @pl.when(source >= 0)
        def _():
            pltpu.make_async_copy(packed_ref.at[jnp.maximum(source, 0)], out_ref.at[s], sem).start()

        @pl.when(source < 0)
        def _():
            pltpu.make_async_copy(zero_ref, out_ref.at[s], sem).start()

    pltpu.make_async_copy(out_ref, out_ref, sem).wait()


def unpack(place, owners, packed, owner_count, direct, half, extra):
    block_rows, width = packed.shape[1:]
    return pl.pallas_call(
        functools.partial(unpack_kernel, owner_count=owner_count, direct=direct, half=half),
        in_specs=[SMEM, SMEM, VMEM],
        out_specs=HBM,
        out_shape=jax.ShapeDtypeStruct((half * extra, block_rows, width), packed.dtype),
        scratch_shapes=[
            pltpu.VMEM((block_rows, width), jnp.bfloat16),
            pltpu.SMEM((half * extra,), jnp.int32),
            pltpu.SMEM((owner_count,), jnp.int32),
            pltpu.SemaphoreType.DMA,
        ],
        compiler_params=pltpu.CompilerParams(vmem_limit_bytes=8 << 20),
        name="unpack",
    )(place, owners, packed)


def gather_kernel(place_ref, near_ref, out_ref, sem, *, half):
    count = near_ref.shape[0]
    base = place_ref[1] // half * count
    copy = pltpu.make_async_copy(near_ref, out_ref.at[pl.ds(base, count)], sem)
    copy.start()
    copy.wait()


def gather(place, near, half):
    count, block_rows, width = near.shape
    return pl.pallas_call(
        functools.partial(gather_kernel, half=half),
        in_specs=[SMEM, VMEM],
        out_specs=HBM,
        out_shape=jax.ShapeDtypeStruct((2 * count, block_rows, width), near.dtype),
        scratch_shapes=[pltpu.SemaphoreType.DMA],
        compiler_params=pltpu.CompilerParams(vmem_limit_bytes=8 << 20),
        name="gather",
    )(place, near)


def finish_kernel(place_ref, proxied_ref, part_ref, *refs, half, cap, direct):
    far_refs, (out_ref, sem) = refs[:half], refs[half:]
    extra = cap - direct
    me = place_ref[1] % half
    base = (1 - place_ref[1] // half) * half
    for j in range(half):
        pltpu.make_async_copy(
            far_refs[j], out_ref.at[pl.ds((base + (me ^ j)) * cap, direct)], sem
        ).start()
        pltpu.make_async_copy(
            proxied_ref.at[pl.ds(j * extra, extra)],
            out_ref.at[pl.ds((base + j) * cap + direct, extra)],
            sem,
        ).start()
    part = out_ref.at[pl.ds(0, half * cap)]
    pltpu.make_async_copy(part, part, sem).wait()


def finish(place, proxied, out, fars, half, cap, direct):
    return pl.pallas_call(
        functools.partial(finish_kernel, half=half, cap=cap, direct=direct),
        in_specs=[SMEM, VMEM, HBM] + [VMEM] * half,
        out_specs=HBM,
        out_shape=jax.ShapeDtypeStruct(out.shape, out.dtype),
        input_output_aliases={2: 0},
        scratch_shapes=[pltpu.SemaphoreType.DMA],
        compiler_params=pltpu.CompilerParams(vmem_limit_bytes=8 << 20),
        name="finish",
    )(place, proxied, out, *fars)


def sizes_of(most):
    return sorted({max(1, most * k // 16) for k in SIZES} | {most})


SIZES = (7, 8, 9, 10, 12)


def body(features, session, owner_map):
    rows, width = features.shape
    blocks = owner_map.shape[1]
    row_count, grp_count = lax.axis_size("row"), lax.axis_size("grp")
    cap = max(1, 2 * blocks // row_count)
    split = cap > 1 and row_count > 2 and row_count & (row_count - 1) == 0
    half = row_count // 2 if split else row_count
    direct = cap * 4 // 8 if split else cap
    extra = cap - direct
    ids = session.reshape(rows // LANES, LANES)
    row, grp = lax.axis_index("row"), lax.axis_index("grp")
    place = jnp.stack([row * grp_count + grp, row])
    everything = lax.all_to_all(
        tails(place, ids, owner_map, features, row_count * grp_count, row_count, direct),
        AXES, split_axis=0, concat_axis=0, tiled=True,
    )
    if not split:
        (sent,) = slotted(
            place, owner_map, ids, everything, features, row_count, cap, direct, half, 0
        )
        return lax.all_to_all(sent, "row", split_axis=0, concat_axis=0, tiled=True)
    groups = [list(range(half)), list(range(half, row_count))]
    most = jnp.max(everything[:, 0, width + 3]).astype(jnp.int32)
    sizes = sizes_of(half * extra)

    def swap(j):
        return [(r, r ^ (half + j)) for r in range(row_count)]

    def exchange(x):
        return lax.all_to_all(
            x, "row", split_axis=0, concat_axis=0, tiled=True, axis_index_groups=groups
        )

    def branch(size):
        def run(place, owner_map, ids, everything, features):
            near, far, packed = slotted(
                place, owner_map, ids, everything, features, row_count, cap, direct, half, size
            )
            packed = lax.ppermute(packed, "row", swap(0))
            near = exchange(near)
            fars = []
            for j in range(half):
                part = far[j * direct : (j + 1) * direct]
                fars.append(lax.ppermute(part, "row", swap(j)))
            other = (place[1] ^ half) * grp_count + grp
            other_owners = lax.dynamic_slice(
                everything, (other, 0, width + LANES), (1, 1, blocks)
            ).reshape(1, blocks).astype(jnp.int32)
            proxied = unpack(place, other_owners, packed, row_count, direct, half, extra)
            proxied = exchange(proxied)
            out = gather(place, near, half)
            return finish(place, proxied, out, fars, half, cap, direct)

        return run

    which = sum((most > size).astype(jnp.int32) for size in sizes[:-1])
    return lax.switch(
        which, [branch(size) for size in sizes],
        place, owner_map, ids, everything, features,
    )


def solution(mesh):
    in_specs = (P(AXES, None), P(AXES), P(AXES, None))
    return jax.shard_map(
        body, mesh=mesh, in_specs=in_specs, out_specs=P(AXES, None, None), check_vma=False
    )
```

time: 126 us -> 134 us (1.063)
  blocking collectives: 97.8 us -> 14.8 us
  waiting for transfers between devices: 7.33 us -> 57.4 us
  starting transfers between devices: 7.33 us -> 33.3 us
  Pallas kernels: 10.4 us -> 17 us
  local copies, waits for them, and re-layouts: 2.62 us -> 9.13 us
    all_to_all x1, blocking collectives: 97.8 us -> 14.8 us  [body(): lax.all_to_all(tails(place, ids, owner_map, features, row_count * grp_cou...]
    ppermute x0 -> x9, waiting for transfers between devices: none -> 57.4 us  [the longest x1 32.3 us: run(): packed = lax.ppermute(packed, 'row', swap(0))]
    ppermute x0 -> x9, starting transfers between devices: none -> 21.8 us  [the longest x8 21.1 us: run(): fars.append(lax.ppermute(part, 'row', swap(j)))]
    cond x0 -> x26, local copies, waits for them, and re-layouts: none -> 7.74 us
    all_to_all x1 -> x2, waiting for transfers between devices: 7.33 us -> 0.01 us  [exchange(): lax.all_to_all(x, 'row', split_axis=0, concat_axis=0, tiled=True, axis_in...]
    pallas_call x2 -> x5, Pallas kernels: 10.4 us -> 17 us  [the longest x1 6.85 us: slotted(): pl.pallas_call(functools.partial(blocks_kernel, owner_count=owner_count,...]
    all_to_all x1 -> x2, starting transfers between devices: 7.33 us -> 11.5 us  [exchange(): lax.all_to_all(x, 'row', split_axis=0, concat_axis=0, tiled=True, axis_in...]
    unnamed x3 -> x4, local copies, waits for them, and re-layouts: 2.62 us -> 0.01 us
  transfers between devices with their start and end apart: 1 -> 11, of which waited for: 1 -> 7; matrix products, arithmetic and copies ran while one was open for 0% -> 1% of each run, Pallas kernels for 0% -> 3%
where the time goes in v3:
time: 134 us; the launch traced here: 133 us
  waiting for transfers between devices  57.4 us (43%)
  starting transfers between devices  33.3 us (25%)
  Pallas kernels  17 us (13%)
  blocking collectives  14.8 us (11%)
  local copies, waits for them, and re-layouts  9.13 us (7%)
    ppermute x1, waiting for transfers between devices, run(): packed = lax.ppermute(packed, 'row', swap(0))  32.3 us
    ppermute x8, waiting for transfers between devices, run(): fars.append(lax.ppermute(part, 'row', swap(j)))  25.1 us
    ppermute x8, starting transfers between devices, run(): fars.append(lax.ppermute(part, 'row', swap(j)))  21.1 us
    all_to_all x1, blocking collectives, body(): lax.all_to_all(tails(place, ids, owner_map, features, row_count * grp_cou...  14.8 us
    all_to_all x2, starting transfers between devices, exchange(): lax.all_to_all(x, 'row', split_axis=0, concat_axis=0, tiled=True, axis_in...  11.5 us
    cond x26, local copies, waits for them, and re-layouts  7.74 us
    pallas_call x1, Pallas kernels, slotted(): pl.pallas_call(functools.partial(blocks_kernel, owner_count=owner_count,...  6.85 us
    pallas_call x1, Pallas kernels, tails(): pl.pallas_call(functools.partial(tail_kernel, row_count=row_count, direct...  3.7 us
  transfers between devices with their start and end apart: 11, of which 7 were waited for; matrix products, arithmetic and copies ran while one was open for 1% of the time, Pallas kernels for 3%

profile of v3, /device:TPU:0, one launch (start us, length us, event | category | flops | bytes accessed | tf_op | source)
XLA Modules:
  0.0 133.3 jit_solution(13854819402879249311)
XLA Ops:
  0.0 0.1 pad_add_fusion.place_ref
  0.1 3.7 %tails.1 = f32[32,1,512]{2,1,0:T(1,128)} custom-call(s32[2]{0:T(128)S(1)} %pad_add_fusion.place_ref, s32[32,128]{1,0:T(8,128)} %bitcast.15, s32[1,64]{1,0:T(1,128)} %owners_ref.1, f32[4096,256]{1,0:T(8,128)} %x_hbm.1), custom_call_target="tpu_custom_call" | custom-call | tf_op jit(solution)/shard_map/tails/pallas_call | solution.py:69
  3.8 14.8 %all_to_all.53 = f32[32,1,512]{2,1,0:T(1,128)S(1)} all-to-all(f32[32,1,512]{2,1,0:T(1,128)} %tails.1), channel_id=1, replica_groups=mesh['row'=16,'grp'=2] {'row','grp'}, dimensions={0} | all-to-all | bytes 131072 | tf_op jit(solution)/shard_map/all_to_all | solution.py:369
  18.5 0.7 slice_reduce_fusion
  19.9 0.0 copy-done.78
  19.9 0.0 copy-done.65
  19.9 113.4 %conditional.1 = (bf16[128,64,256]{2,1,0:T(8,128)(2,1)}) conditional(s32[]{:T(128)} %clamp.3, (s32[]{:T(128)}, s32[]{:T(128)}, f32[32,1,512]{2,1,0:T(1,128)S(1)}, s32[2]{0:T(128)S(1)}, s32[1,64]{1,0:T(1,128)S(1)}, /*index=5*/s32[32,128]{1,0:T(8,128)S(1)}, f32[4096,256]{1,0:T(8,128)}) %tuple.84, (s32[]{:T(128)}, ...), branch_computations={%region_1.0_spmd, %region_2.0_spmd, %region_3.0_spmd, %region_4.0_... | conditional | flops 70 | bytes 26478018 | solution.py:413
  19.9 0.0 copy-start.66
  20.0 6.9 %slotted.6 = (bf16[64,64,256]{2,1,0:T(8,128)(2,1)}, bf16[32,64,256]{2,1,0:T(8,128)(2,1)}, bf16[14,64,256]{2,1,0:T(8,128)(2,1)}) custom-call(s32[2]{0:T(128)S(1)} %get-tuple-element.84.place_ref, s32[1,64]{1,0:T(1,128)S(1)} %get-tuple-element.100.owners_ref, s32[32,128]{1,0:T(8,128)S(1)} %get-tuple-element.101.ids_ref, ...), custom_call_target="tpu_custom_call" | custom-call | tf_op jit(solution)/shard_map/cond/branch_0_fun/slotted/pallas_call | solution.py:221
  26.8 3.7 %all-to-all-start.1 = ((bf16[64,64,256]{2,1,0:T(8,128)(2,1)}), bf16[64,64,256]{2,1,0:T(8,128)(2,1)S(1)}, u32[]{:S(2)}, u32[]{:S(2)}) async-start(bf16[64,64,256]{2,1,0:T(8,128)(2,1)} %get-tuple-element.104), calls=%async_computation.1 | async-start | bytes 4194304 | tf_op jit(solution)/shard_map/cond/branch_0_fun/all_to_all | solution.py:386
  30.6 0.0 copy-done.82
  30.6 0.7 collective-permute-start
  31.3 32.3 %collective-permute-done.packed_ref = bf16[14,64,256]{2,1,0:T(8,128)(2,1)S(1)} collective-permute-done((bf16[14,64,256]{2,1,0:T(8,128)(2,1)S(1)}, bf16[14,64,256]{2,1,0:T(8,128)(2,1)S(1)}, u32[]{:S(2)}, u32[]{:S(2)}) %collective-permute-start) | collective-permute-done | bytes 458784 | tf_op jit(solution)/shard_map/cond/branch_0_fun/ppermute | solution.py:395
  63.7 0.0 copy-done.66
  63.7 2.7 %unpack.6 = bf16[32,64,256]{2,1,0:T(8,128)(2,1)} custom-call(s32[2]{0:T(128)S(1)} %get-tuple-element.84.place_ref, s32[1,64]{1,0:T(1,128)S(1)} %convert_bitcast_fusion.owners_ref, bf16[14,64,256]{2,1,0:T(8,128)(2,1)S(1)} %collective-permute-done.packed_ref), custom_call_target="tpu_custom_call" | custom-call | tf_op jit(solution)/shard_map/cond/branch_0_fun/unpack/pallas_call | solution.py:282
  66.4 0.0 copy-start.67
  66.4 0.0 all-to-all-done.1.near_ref
  66.4 7.8 %all-to-all-start = ((bf16[32,64,256]{2,1,0:T(8,128)(2,1)}), bf16[32,64,256]{2,1,0:T(8,128)(2,1)S(1)}, u32[]{:S(2)}, u32[]{:S(2)}) async-start(bf16[32,64,256]{2,1,0:T(8,128)(2,1)} %unpack.6), calls=%async_computation | async-start | bytes 2097152 | tf_op jit(solution)/shard_map/cond/branch_0_fun/all_to_all | solution.py:386
  74.2 1.4 %fusion = (bf16[4,64,256]{2,1,0:T(8,128)(2,1)S(1)}, bf16[4,64,256]{2,1,0:T(8,128)(2,1)S(1)}, bf16[4,64,256]{2,1,0:T(8,128)(2,1)S(1)}, bf16[4,64,256]{2,1,0:T(8,1...) fusion(bf16[32,64,256]{2,1,0:T(8,128)(2,1)} %get-tuple-element.105), kind=kLoop, calls=%fused_computation.8 | loop fusion | bytes 2097152 | tf_op jit(solution)/shard_map/cond/branch_0_fun/slice | solution.py:399
  75.6 6.2 %collective-permute-start.8 = (bf16[4,64,256]{2,1,0:T(8,128)(2,1)S(1)}, bf16[4,64,256]{2,1,0:T(8,128)(2,1)S(1)}, u32[]{:S(2)}, u32[]{:S(2)}) collective-permute-start(bf16[4,64,256]{2,1,0:T(8,128)(2,1)S(1)} %get-tuple-element.157), channel_id=1, source_target_pairs={{0,30},{2,28},{4,26},{6,24},{8,22},{10,20},{12,18},{14,16},{16,14}... | collective-permute-start | bytes 393224 | tf_op jit(solution)/shard_map/cond/branch_0_fun/ppermute | solution.py:400
  81.8 0.0 collective-permute-start.7
  81.8 3.8 %collective-permute-start.6 = (bf16[4,64,256]{2,1,0:T(8,128)(2,1)S(1)}, bf16[4,64,256]{2,1,0:T(8,128)(2,1)S(1)}, u32[]{:S(2)}, u32[]{:S(2)}) collective-permute-start(bf16[4,64,256]{2,1,0:T(8,128)(2,1)S(1)} %get-tuple-element.159), channel_id=1, source_target_pairs={{0,26},{2,24},{4,30},{6,28},{8,18},{10,16},{12,22},{14,20},{16,10}... | collective-permute-start | bytes 393224 | tf_op jit(solution)/shard_map/cond/branch_0_fun/ppermute | solution.py:400
  85.6 0.1 collective-permute-start.5
  85.7 1.0 collective-permute-start.4
  86.8 11.0 %collective-permute-done.8.refs_7_ = bf16[4,64,256]{2,1,0:T(8,128)(2,1)S(1)} collective-permute-done((bf16[4,64,256]{2,1,0:T(8,128)(2,1)S(1)}, bf16[4,64,256]{2,1,0:T(8,128)(2,1)S(1)}, u32[]{:S(2)}, u32[]{:S(2)}) %collective-permute-start.8) | collective-permute-done | bytes 131104 | tf_op jit(solution)/shard_map/cond/branch_0_fun/ppermute | solution.py:400
  97.7 0.0 collective-permute-start.3
  97.7 3.5 %collective-permute-done.7.refs_6_ = bf16[4,64,256]{2,1,0:T(8,128)(2,1)S(1)} collective-permute-done((bf16[4,64,256]{2,1,0:T(8,128)(2,1)S(1)}, bf16[4,64,256]{2,1,0:T(8,128)(2,1)S(1)}, u32[]{:S(2)}, u32[]{:S(2)}) %collective-permute-start.7) | collective-permute-done | bytes 131104 | tf_op jit(solution)/shard_map/cond/branch_0_fun/ppermute | solution.py:400
  101.3 0.0 collective-permute-start.2
  101.3 1.1 collective-permute-done.6.refs_5_
  102.4 9.9 %collective-permute-start.1 = (bf16[4,64,256]{2,1,0:T(8,128)(2,1)S(1)}, bf16[4,64,256]{2,1,0:T(8,128)(2,1)S(1)}, u32[]{:S(2)}, u32[]{:S(2)}) collective-permute-start(bf16[4,64,256]{2,1,0:T(8,128)(2,1)S(1)} %get-tuple-element.164), channel_id=1, source_target_pairs={{0,16},{2,18},{4,20},{6,22},{8,24},{10,26},{12,28},{14,30},{16,0},... | collective-permute-start | bytes 393224 | tf_op jit(solution)/shard_map/cond/branch_0_fun/ppermute | solution.py:400
  112.3 1.9 %gather.6.part_ref = bf16[128,64,256]{2,1,0:T(8,128)(2,1)} custom-call(s32[2]{0:T(128)S(1)} %copy-done.67, bf16[64,64,256]{2,1,0:T(8,128)(2,1)S(1)} %all-to-all-done.1.near_ref), custom_call_target="tpu_custom_call" | custom-call | tf_op jit(solution)/shard_map/cond/branch_0_fun/gather/pallas_call | solution.py:308
  114.2 0.0 collective-permute-done.5.refs_4_
  114.2 0.6 copy-done
  114.8 5.8 %collective-permute-done.4.refs_3_ = bf16[4,64,256]{2,1,0:T(8,128)(2,1)S(1)} collective-permute-done((bf16[4,64,256]{2,1,0:T(8,128)(2,1)S(1)}, bf16[4,64,256]{2,1,0:T(8,128)(2,1)S(1)}, u32[]{:S(2)}, u32[]{:S(2)}) %collective-permute-start.4) | collective-permute-done | bytes 131104 | tf_op jit(solution)/shard_map/cond/branch_0_fun/ppermute | solution.py:400
  120.7 0.6 copy-done.12
  121.3 2.3 %collective-permute-done.3.refs_2_ = bf16[4,64,256]{2,1,0:T(8,128)(2,1)S(1)} collective-permute-done((bf16[4,64,256]{2,1,0:T(8,128)(2,1)S(1)}, bf16[4,64,256]{2,1,0:T(8,128)(2,1)S(1)}, u32[]{:S(2)}, u32[]{:S(2)}) %collective-permute-start.3) | collective-permute-done | bytes 131104 | tf_op jit(solution)/shard_map/cond/branch_0_fun/ppermute | solution.py:400
  123.6 0.6 copy-done.24
  124.2 1.4 %collective-permute-done.2.refs_1_ = bf16[4,64,256]{2,1,0:T(8,128)(2,1)S(1)} collective-permute-done((bf16[4,64,256]{2,1,0:T(8,128)(2,1)S(1)}, bf16[4,64,256]{2,1,0:T(8,128)(2,1)S(1)}, u32[]{:S(2)}, u32[]{:S(2)}) %collective-permute-start.2) | collective-permute-done | bytes 131104 | tf_op jit(solution)/shard_map/cond/branch_0_fun/ppermute | solution.py:400
  125.6 0.6 copy-done.36
  126.2 0.0 collective-permute-done.1.refs_0_
  126.2 0.6 copy-done.48
  126.9 0.0 all-to-all-done.proxied_ref
  126.9 0.9 copy-done.1
  127.8 0.9 copy-done.13
  128.7 0.9 copy-done.25
  129.6 0.9 copy-done.37
  130.5 0.9 copy-done.49
  131.4 1.9 %finish.6 = bf16[128,64,256]{2,1,0:T(8,128)(2,1)} custom-call(s32[2]{0:T(128)S(1)} %copy-done.67, bf16[32,64,256]{2,1,0:T(8,128)(2,1)S(1)} %all-to-all-done.proxied_ref, bf16[128,64,256]{2,1,0:T(8,128)(2,1)} %gather.6.part_ref, bf16[4,64,256]{2,1,0:T(8,128)(2,1)S(1)} %copy-done.49, ...), custom_call_target="tpu_custom_call", output_to_operand_aliasing={{}: (2, {})} | custom-call | tf_op jit(solution)/shard_map/cond/branch_0_fun/finish/pallas_call | solution.py:338
  (15 shorter events, 0.0 us)
Async XLA Ops:
  0.0 19.9 %copy-start.78 = (s32[1,64]{1,0:T(1,128)S(1)}, s32[1,64]{1,0:T(1,128)}, u32[]{:S(2)}) copy-start(s32[1,64]{1,0:T(1,128)} %owners_ref.1) | copy-start | bytes 772
  0.0 19.9 %copy-start.65 = (s32[4096]{0:T(1024)S(1)}, s32[4096]{0:T(1024)}, u32[]{:S(2)}) copy-start(s32[4096]{0:T(1024)} %param.10) | copy-start | bytes 49156
  19.9 43.7 %copy-start.66 = (s32[2]{0:T(128)}, s32[2]{0:T(128)S(1)}, u32[]{:S(2)}) copy-start(s32[2]{0:T(128)S(1)} %get-tuple-element.84.place_ref) | copy-start | bytes 28 | tf_op jit(solution)/shard_map/cond
  26.8 3.8 %copy-start.82 = (bf16[14,64,256]{2,1,0:T(8,128)(2,1)S(1)}, bf16[14,64,256]{2,1,0:T(8,128)(2,1)}, u32[]{:S(2)}) copy-start(bf16[14,64,256]{2,1,0:T(8,128)(2,1)} %get-tuple-element.103) | copy-start | bytes 1376260 | tf_op jit(solution)/shard_map/cond
  26.8 39.6 %all-to-all-start.1 = ((bf16[64,64,256]{2,1,0:T(8,128)(2,1)}), bf16[64,64,256]{2,1,0:T(8,128)(2,1)S(1)}, u32[]{:S(2)}, u32[]{:S(2)}) async-start(bf16[64,64,256]{2,1,0:T(8,128)(2,1)} %get-tuple-element.104), calls=%async_computation.1 | async-start | bytes 4194304 | tf_op jit(solution)/shard_map/cond/branch_0_fun/all_to_all | solution.py:386
  30.6 33.1 %collective-permute-start = (bf16[14,64,256]{2,1,0:T(8,128)(2,1)S(1)}, bf16[14,64,256]{2,1,0:T(8,128)(2,1)S(1)}, u32[]{:S(2)}, u32[]{:S(2)}) collective-permute-start(bf16[14,64,256]{2,1,0:T(8,128)(2,1)S(1)} %copy-done.82), channel_id=1, source_target_pairs={{0,16},{2,18},{4,20},{6,22},{8,24},{10,26},{12,28},{14,30},{16,0},... | collective-permute-start | bytes 1376264 | tf_op jit(solution)/shard_map/cond/branch_0_fun/ppermute | solution.py:395
  66.4 45.9 %copy-start.67 = (s32[2]{0:T(128)S(1)}, s32[2]{0:T(128)}, u32[]{:S(2)}) copy-start(s32[2]{0:T(128)} %copy-done.66) | copy-start | bytes 28 | tf_op jit(solution)/shard_map/cond
  66.4 60.5 %all-to-all-start = ((bf16[32,64,256]{2,1,0:T(8,128)(2,1)}), bf16[32,64,256]{2,1,0:T(8,128)(2,1)S(1)}, u32[]{:S(2)}, u32[]{:S(2)}) async-start(bf16[32,64,256]{2,1,0:T(8,128)(2,1)} %unpack.6), calls=%async_computation | async-start | bytes 2097152 | tf_op jit(solution)/shard_map/cond/branch_0_fun/all_to_all | solution.py:386
  75.6 22.1 %collective-permute-start.8 = (bf16[4,64,256]{2,1,0:T(8,128)(2,1)S(1)}, bf16[4,64,256]{2,1,0:T(8,128)(2,1)S(1)}, u32[]{:S(2)}, u32[]{:S(2)}) collective-permute-start(bf16[4,64,256]{2,1,0:T(8,128)(2,1)S(1)} %get-tuple-element.157), channel_id=1, source_target_pairs={{0,30},{2,28},{4,26},{6,24},{8,22},{10,20},{12,18},{14,16},{16,14}... | collective-permute-start | bytes 393224 | tf_op jit(solution)/shard_map/cond/branch_0_fun/ppermute | solution.py:400
  81.8 19.4 %collective-permute-start.7 = (bf16[4,64,256]{2,1,0:T(8,128)(2,1)S(1)}, bf16[4,64,256]{2,1,0:T(8,128)(2,1)S(1)}, u32[]{:S(2)}, u32[]{:S(2)}) collective-permute-start(bf16[4,64,256]{2,1,0:T(8,128)(2,1)S(1)} %get-tuple-element.158), channel_id=1, source_target_pairs={{0,28},{2,30},{4,24},{6,26},{8,20},{10,22},{12,16},{14,18},{16,12}... | collective-permute-start | bytes 393224 | tf_op jit(solution)/shard_map/cond/branch_0_fun/ppermute | solution.py:400
  81.8 20.6 %collective-permute-start.6 = (bf16[4,64,256]{2,1,0:T(8,128)(2,1)S(1)}, bf16[4,64,256]{2,1,0:T(8,128)(2,1)S(1)}, u32[]{:S(2)}, u32[]{:S(2)}) collective-permute-start(bf16[4,64,256]{2,1,0:T(8,128)(2,1)S(1)} %get-tuple-element.159), channel_id=1, source_target_pairs={{0,26},{2,24},{4,30},{6,28},{8,18},{10,16},{12,22},{14,20},{16,10}... | collective-permute-start | bytes 393224 | tf_op jit(solution)/shard_map/cond/branch_0_fun/ppermute | solution.py:400
  85.6 28.5 %collective-permute-start.5 = (bf16[4,64,256]{2,1,0:T(8,128)(2,1)S(1)}, bf16[4,64,256]{2,1,0:T(8,128)(2,1)S(1)}, u32[]{:S(2)}, u32[]{:S(2)}) collective-permute-start(bf16[4,64,256]{2,1,0:T(8,128)(2,1)S(1)} %get-tuple-element.160), channel_id=1, source_target_pairs={{0,24},{2,26},{4,28},{6,30},{8,16},{10,18},{12,20},{14,22},{16,8},... | collective-permute-start | bytes 393224 | tf_op jit(solution)/shard_map/cond/branch_0_fun/ppermute | solution.py:400
  85.7 34.9 %collective-permute-start.4 = (bf16[4,64,256]{2,1,0:T(8,128)(2,1)S(1)}, bf16[4,64,256]{2,1,0:T(8,128)(2,1)S(1)}, u32[]{:S(2)}, u32[]{:S(2)}) collective-permute-start(bf16[4,64,256]{2,1,0:T(8,128)(2,1)S(1)} %get-tuple-element.161), channel_id=1, source_target_pairs={{0,22},{2,20},{4,18},{6,16},{8,30},{10,28},{12,26},{14,24},{16,6},... | collective-permute-start | bytes 393224 | tf_op jit(solution)/shard_map/cond/branch_0_fun/ppermute | solution.py:400
  97.7 25.8 %collective-permute-start.3 = (bf16[4,64,256]{2,1,0:T(8,128)(2,1)S(1)}, bf16[4,64,256]{2,1,0:T(8,128)(2,1)S(1)}, u32[]{:S(2)}, u32[]{:S(2)}) collective-permute-start(bf16[4,64,256]{2,1,0:T(8,128)(2,1)S(1)} %get-tuple-element.162), channel_id=1, source_target_pairs={{0,20},{2,22},{4,16},{6,18},{8,28},{10,30},{12,24},{14,26},{16,4},... | collective-permute-start | bytes 393224 | tf_op jit(solution)/shard_map/cond/branch_0_fun/ppermute | solution.py:400
  101.3 24.3 %collective-permute-start.2 = (bf16[4,64,256]{2,1,0:T(8,128)(2,1)S(1)}, bf16[4,64,256]{2,1,0:T(8,128)(2,1)S(1)}, u32[]{:S(2)}, u32[]{:S(2)}) collective-permute-start(bf16[4,64,256]{2,1,0:T(8,128)(2,1)S(1)} %get-tuple-element.163), channel_id=1, source_target_pairs={{0,18},{2,16},{4,22},{6,20},{8,26},{10,24},{12,30},{14,28},{16,2},... | collective-permute-start | bytes 393224 | tf_op jit(solution)/shard_map/cond/branch_0_fun/ppermute | solution.py:400
  102.4 23.8 %collective-permute-start.1 = (bf16[4,64,256]{2,1,0:T(8,128)(2,1)S(1)}, bf16[4,64,256]{2,1,0:T(8,128)(2,1)S(1)}, u32[]{:S(2)}, u32[]{:S(2)}) collective-permute-start(bf16[4,64,256]{2,1,0:T(8,128)(2,1)S(1)} %get-tuple-element.164), channel_id=1, source_target_pairs={{0,16},{2,18},{4,20},{6,22},{8,24},{10,26},{12,28},{14,30},{16,0},... | collective-permute-start | bytes 393224 | tf_op jit(solution)/shard_map/cond/branch_0_fun/ppermute | solution.py:400
  114.2 0.6 copy-start
  120.7 0.6 copy-start.12
  123.6 0.6 copy-start.24
  125.6 0.6 copy-start.36
  126.2 0.6 copy-start.48
  126.9 0.9 copy-start.1
  127.8 0.9 copy-start.13
  128.7 0.9 copy-start.25
  129.6 0.9 copy-start.37
  130.5 0.9 copy-start.49

commit v4 on v3

v4 whole, which is shorter than its diff:
```python
import functools

import jax
import jax.numpy as jnp
from jax import lax
from jax.experimental import pallas as pl
from jax.experimental.pallas import tpu as pltpu
from jax.sharding import PartitionSpec as P


LANES = 128
AXES = ("row", "grp")
PIECES = 8
VMEM = pl.BlockSpec(memory_space=pltpu.VMEM)
SMEM = pl.BlockSpec(memory_space=pltpu.SMEM)
ANY = pl.BlockSpec(memory_space=pl.ANY)
HBM = pl.BlockSpec(memory_space=pltpu.HBM)


def piece_copy(hbm_ref, vmem_ref, sem_ref, piece):
    rows = hbm_ref.shape[0] // PIECES
    part = pl.ds(pl.multiple_of(piece * rows, rows), rows)
    return pltpu.make_async_copy(hbm_ref.at[part], vmem_ref.at[part], sem_ref.at[piece])


def here():
    row, grp = lax.axis_index("row"), lax.axis_index("grp")
    return row * lax.axis_size("grp") + grp, row


def loaded(copies):
    for copy in copies:
        copy.start()
    return copies


def column(row, size):
    return jnp.broadcast_to(row.astype(jnp.float32), (size, row.shape[1])).T.astype(jnp.int32)


def padded(row):
    return jnp.concatenate([row, jnp.zeros((1, LANES - row.shape[1]), row.dtype)], axis=1)


def tail_kernel(
    ids_hbm, owners_hbm, x_hbm, out_ref, table_ref, ids_ref, owners_ref, x_ref, sem_ref,
    *, row_count, cap, direct, half
):
    rows, width = x_ref.shape
    chunk = rows // PIECES
    small = loaded([
        pltpu.make_async_copy(ids_hbm, ids_ref, sem_ref.at[PIECES]),
        pltpu.make_async_copy(owners_hbm, owners_ref, sem_ref.at[PIECES + 1]),
    ])
    for piece in range(PIECES):
        piece_copy(x_hbm, x_ref, sem_ref, piece).start()
    my_row = here()[1]
    for copy in small:
        copy.wait()
    ids = ids_ref[...]
    id_rows = ids.shape[0]
    last = ids_ref[id_rows - 1 : id_rows, LANES - 1 : LANES]
    in_tail = jnp.where(ids == last, 1, 0)
    count = jnp.sum(jnp.sum(in_tail, axis=0, keepdims=True), axis=1, keepdims=True)

    blocks = owners_ref.shape[1]
    extra = cap - direct
    owners = padded(owners_ref[...])
    by_block = column(owners, LANES)
    block = lax.broadcasted_iota(jnp.int32, (LANES, LANES), 0)
    lane = lax.broadcasted_iota(jnp.int32, (LANES, LANES), 1)
    before = (block < lane) & (block < blocks)
    rank = jnp.sum(jnp.where(before & (by_block == owners), 1, 0), axis=0, keepdims=True)
    used = jnp.sum(jnp.where((by_block == lane) & (block < blocks), 1, 0), axis=0, keepdims=True)
    local = owners % half
    near = local * cap + rank
    if half < row_count:
        across = owners // half != my_row // half
        over = across & (rank >= direct) & (lane[:1] < blocks)
        over_by_block = column(jnp.where(over, 1, 0), LANES)
        packed = jnp.sum(jnp.where(before, over_by_block, 0), axis=0, keepdims=True)
        total_packed = jnp.sum(jnp.where(over, 1, 0), axis=1, keepdims=True)
        far = half * cap + (local ^ (my_row % half)) * direct + rank
        code = jnp.where(over, half * (cap + direct) + packed, jnp.where(across, far, near))
        goes = column(jnp.where(over, local * extra + rank - direct, -1), LANES)
        comes = jnp.where(goes == lane, column(packed, LANES) + 1, 0)
        source = jnp.sum(comes, axis=0, keepdims=True) - 1
    else:
        code, source, total_packed = near, rank, jnp.zeros_like(count)
    table_ref[0:1, :] = code
    table_ref[1:2, :] = used
    table_ref[2:3, :] = jnp.broadcast_to(total_packed, (1, LANES))

    lane = lane[:1]
    meta = jnp.where(lane == 2, count, total_packed)
    meta = jnp.where(lane == 0, ids_ref[0:1, 0:1], jnp.where(lane == 1, last, meta))
    row = lax.broadcasted_iota(jnp.int32, (chunk, width), 0)

    def add(piece, total):
        piece_copy(x_hbm, x_ref, sem_ref, piece).wait()
        part = x_ref[pl.ds(pl.multiple_of(piece * chunk, chunk), chunk), :]
        kept = jnp.where(row >= rows - count - piece * chunk, part, 0.0)
        return total + jnp.sum(kept.reshape(chunk // 8, 8, width), axis=0)

    total = lax.fori_loop(0, PIECES, add, jnp.zeros((8, width), jnp.float32))
    tail = jnp.sum(total, axis=0, keepdims=True)
    message = jnp.concatenate(
        [tail, meta.astype(jnp.float32), source.astype(jnp.float32)], axis=1
    )
    out_ref[...] = jnp.broadcast_to(message[None], out_ref.shape)


def tails(ids, owners, features, copies, row_count, cap, direct, half):
    rows, width = features.shape
    return pl.pallas_call(
        functools.partial(tail_kernel, row_count=row_count, cap=cap, direct=direct, half=half),
        in_specs=[ANY, ANY, ANY],
        out_specs=[VMEM, VMEM],
        out_shape=[
            jax.ShapeDtypeStruct((copies, 1, width + 2 * LANES), jnp.float32),
            jax.ShapeDtypeStruct((3, LANES), jnp.int32),
        ],
        scratch_shapes=[
            pltpu.VMEM(ids.shape, ids.dtype),
            pltpu.VMEM(owners.shape, owners.dtype),
            pltpu.VMEM((rows, width), jnp.float32),
            pltpu.SemaphoreType.DMA((PIECES + 2,)),
        ],
        name="tails",
    )(ids, owners, features)


def blocks_kernel(
    table_hbm, ids_hbm, all_hbm, x_hbm, *refs, owner_count, cap, direct, half
):
    outs, scratch = refs[:-8], refs[-8:]
    table_ref, ids_ref, all_ref, x_ref, norm_ref, zero_ref, sem_ref, done_ref = scratch
    rows, width = x_ref.shape
    _, block_rows, _ = norm_ref.shape
    tile = LANES
    chunk = rows // PIECES
    tiles = chunk // tile
    small = loaded([
        pltpu.make_async_copy(table_hbm, table_ref, sem_ref.at[PIECES]),
        pltpu.make_async_copy(ids_hbm, ids_ref, sem_ref.at[PIECES + 1]),
        pltpu.make_async_copy(all_hbm, all_ref, sem_ref.at[PIECES + 2]),
    ])
    for piece in range(PIECES):
        piece_copy(x_hbm, x_ref, sem_ref, piece).start()
    zero_ref[...] = jnp.zeros_like(zero_ref)
    firsts = [0, half * cap, half * (cap + direct)]
    my_device, my_row = here()
    my_half, me = my_row // half, my_row % half
    for copy in small:
        copy.wait()

    def clear(kind, slot):
        pltpu.make_async_copy(zero_ref, outs[kind].at[slot], done_ref.at[kind]).start()

    @pl.loop(0, half)
    def _(o):
        @pl.loop(table_ref[1, my_half * half + o], cap)
        def _(k):
            clear(0, o * cap + k)

    if half < owner_count:
        @pl.loop(0, half)
        def _(o):
            @pl.loop(jnp.minimum(table_ref[1, (1 - my_half) * half + o], direct), direct)
            def _(k):
                clear(1, (o ^ me) * direct + k)

        @pl.loop(table_ref[2, 0], outs[2].shape[0])
        def _(k):
            clear(2, k)

    def send(b):
        code = table_ref[0, b]
        for kind in range(len(outs)):
            inside = code >= firsts[kind]
            if kind + 1 < len(outs):
                inside = inside & (code < firsts[kind + 1])

            @pl.when(inside)
            def _():
                pltpu.make_async_copy(
                    norm_ref.at[b], outs[kind].at[code - firsts[kind]], done_ref.at[kind]
                ).start()

    everything = all_ref[:, 0, :]
    first = ids_ref[0:1, 0:1].astype(jnp.float32)
    device = lax.broadcasted_iota(jnp.int32, (everything.shape[0], 1), 0)
    feeds = (device < my_device) & (everything[:, width + 1 : width + 2] == first)
    carry = jnp.sum(jnp.where(feeds, everything[:, :width], 0.0), axis=0, keepdims=True)
    carry_count = jnp.sum(
        jnp.where(feeds, everything[:, width + 2 : width + 3], 0.0), axis=0, keepdims=True
    )
    carry_count = jnp.broadcast_to(carry_count, (1, LANES))

    lower = lax.broadcasted_iota(jnp.int32, (tile, tile), 1) <= lax.broadcasted_iota(
        jnp.int32, (tile, tile), 0
    )
    ones = jnp.ones((tile, LANES), jnp.bfloat16)
    row = lax.broadcasted_iota(jnp.int32, (tile, LANES), 0)

    def run(piece, carried):
        carry, carry_count, before = carried
        piece_copy(x_hbm, x_ref, sem_ref, piece).wait()
        for k in range(tiles):
            t = piece * tiles + k
            id_row = ids_ref[pl.ds(t, 1), :].astype(jnp.float32)
            ids = jnp.broadcast_to(id_row, (tile, tile))
            same = (ids == ids.T) & lower
            mask = jnp.where(same, 1.0, 0.0).astype(jnp.bfloat16)
            x = x_ref[pl.ds(pl.multiple_of(t * tile, tile), tile), :]
            high = x.astype(jnp.bfloat16)
            rest = x - high.astype(jnp.float32)
            middle = rest.astype(jnp.bfloat16)
            low = (rest - middle.astype(jnp.float32)).astype(jnp.bfloat16)
            count = jnp.dot(mask, ones, preferred_element_type=jnp.float32)
            twice = jnp.concatenate([mask, mask], axis=1)
            both = jnp.concatenate([high, middle], axis=0)
            total = jnp.dot(mask, low, preferred_element_type=jnp.float32) + jnp.dot(
                twice, both, preferred_element_type=jnp.float32
            )
            joined = jnp.sum(jnp.where(id_row == before, 1, 0), axis=1, keepdims=True)
            follows = row < joined
            follows_wide = jnp.concatenate([follows] * (width // LANES), axis=1)
            total = total + jnp.where(follows_wide, carry, 0.0)
            count = count + jnp.where(follows, carry_count, 0.0)
            carry = total[tile - 1 :, :]
            carry_count = count[tile - 1 :, :]
            before = id_row[:, LANES - 1 :]
            scale = lax.rsqrt(count)
            value = (total * jnp.concatenate([scale] * (width // LANES), axis=1)).astype(jnp.bfloat16)
            per_tile = tile // block_rows
            for p in range(per_tile):
                b = t * per_tile + p
                norm_ref[b] = value[p * block_rows : (p + 1) * block_rows, :]
                send(b)
        return carry, carry_count, before

    lax.fori_loop(0, PIECES, run, (carry, carry_count, first))
    for kind, out in enumerate(outs):
        pltpu.make_async_copy(out, out, done_ref.at[kind]).wait()


def slotted(table, ids, everything, features, blocks, owner_count, cap, direct, half, size):
    rows, width = features.shape
    block_rows = rows // blocks
    counts = [half * cap] + ([half * direct, size] if half < owner_count else [])
    return pl.pallas_call(
        functools.partial(
            blocks_kernel, owner_count=owner_count, cap=cap, direct=direct, half=half
        ),
        in_specs=[ANY] * 4,
        out_specs=[HBM] * len(counts),
        out_shape=[jax.ShapeDtypeStruct((n, block_rows, width), jnp.bfloat16) for n in counts],
        scratch_shapes=[
            pltpu.SMEM(table.shape, table.dtype),
            pltpu.VMEM(ids.shape, ids.dtype),
            pltpu.VMEM(everything.shape, everything.dtype),
            pltpu.VMEM((rows, width), jnp.float32),
            pltpu.VMEM((blocks, block_rows, width), jnp.bfloat16),
            pltpu.VMEM((block_rows, width), jnp.bfloat16),
            pltpu.SemaphoreType.DMA((PIECES + 3,)),
            pltpu.SemaphoreType.DMA((3,)),
        ],
        name="slotted",
    )(table, ids, everything, features)


def unpack_kernel(source_ref, packed_ref, out_ref, zero_ref, sem):
    zero_ref[...] = jnp.zeros_like(zero_ref)

    @pl.loop(0, out_ref.shape[0])
    def _(s):
        source = source_ref[0, s]

        @pl.when(source >= 0)
        def _():
            pltpu.make_async_copy(packed_ref.at[jnp.maximum(source, 0)], out_ref.at[s], sem).start()

        @pl.when(source < 0)
        def _():
            pltpu.make_async_copy(zero_ref, out_ref.at[s], sem).start()

    pltpu.make_async_copy(out_ref, out_ref, sem).wait()


def unpack(source, packed, count):
    block_rows, width = packed.shape[1:]
    return pl.pallas_call(
        unpack_kernel,
        in_specs=[SMEM, VMEM],
        out_specs=HBM,
        out_shape=jax.ShapeDtypeStruct((count, block_rows, width), packed.dtype),
        scratch_shapes=[
            pltpu.VMEM((block_rows, width), jnp.bfloat16),
            pltpu.SemaphoreType.DMA,
        ],
        compiler_params=pltpu.CompilerParams(vmem_limit_bytes=8 << 20),
        name="unpack",
    )(source, packed)


def gather_kernel(near_ref, out_ref, sem, *, half):
    count = near_ref.shape[0]
    base = here()[1] // half * count
    copy = pltpu.make_async_copy(near_ref, out_ref.at[pl.ds(base, count)], sem)
    copy.start()
    copy.wait()


def gather(near, half):
    count, block_rows, width = near.shape
    return pl.pallas_call(
        functools.partial(gather_kernel, half=half),
        in_specs=[VMEM],
        out_specs=HBM,
        out_shape=jax.ShapeDtypeStruct((2 * count, block_rows, width), near.dtype),
        scratch_shapes=[pltpu.SemaphoreType.DMA],
        compiler_params=pltpu.CompilerParams(vmem_limit_bytes=8 << 20),
        name="gather",
    )(near)


def finish_kernel(proxied_ref, part_ref, *refs, half, cap, direct):
    far_refs, (out_ref, sem) = refs[:half], refs[half:]
    extra = cap - direct
    my_row = here()[1]
    me = my_row % half
    base = (1 - my_row // half) * half
    for j in range(half):
        pltpu.make_async_copy(
            far_refs[j], out_ref.at[pl.ds((base + (me ^ j)) * cap, direct)], sem
        ).start()
        pltpu.make_async_copy(
            proxied_ref.at[pl.ds(j * extra, extra)],
            out_ref.at[pl.ds((base + j) * cap + direct, extra)],
            sem,
        ).start()
    part = out_ref.at[pl.ds(0, half * cap)]
    pltpu.make_async_copy(part, part, sem).wait()


def finish(proxied, out, fars, half, cap, direct):
    return pl.pallas_call(
        functools.partial(finish_kernel, half=half, cap=cap, direct=direct),
        in_specs=[VMEM, HBM] + [VMEM] * half,
        out_specs=HBM,
        out_shape=jax.ShapeDtypeStruct(out.shape, out.dtype),
        input_output_aliases={1: 0},
        scratch_shapes=[pltpu.SemaphoreType.DMA],
        compiler_params=pltpu.CompilerParams(vmem_limit_bytes=8 << 20),
        name="finish",
    )(proxied, out, *fars)


def sizes_of(most):
    return sorted({max(1, most * k // 16) for k in SIZES} | {most})


SIZES = (7, 8, 9, 10, 12)


def body(features, session, owner_map):
    rows, width = features.shape
    blocks = owner_map.shape[1]
    row_count, grp_count = lax.axis_size("row"), lax.axis_size("grp")
    cap = max(1, 2 * blocks // row_count)
    split = cap > 1 and row_count > 2 and row_count & (row_count - 1) == 0
    half = row_count // 2 if split else row_count
    direct = cap * 4 // 8 if split else cap
    extra = cap - direct
    ids = session.reshape(rows // LANES, LANES)
    row, grp = lax.axis_index("row"), lax.axis_index("grp")
    message, table = tails(
        ids, owner_map, features, row_count * grp_count, row_count, cap, direct, half
    )
    everything = lax.all_to_all(message, AXES, split_axis=0, concat_axis=0, tiled=True)
    if not split:
        (sent,) = slotted(
            table, ids, everything, features, blocks, row_count, cap, direct, half, 0
        )
        return lax.all_to_all(sent, "row", split_axis=0, concat_axis=0, tiled=True)
    groups = [list(range(half)), list(range(half, row_count))]
    most = jnp.max(everything[:, 0, width + 3]).astype(jnp.int32)
    sizes = sizes_of(half * extra)

    def swap(j):
        return [(r, r ^ (half + j)) for r in range(row_count)]

    def exchange(x):
        return lax.all_to_all(
            x, "row", split_axis=0, concat_axis=0, tiled=True, axis_index_groups=groups
        )

    def branch(size):
        def run(table, ids, everything, features):
            near, far, packed = slotted(
                table, ids, everything, features, blocks, row_count, cap, direct, half, size
            )
            packed = lax.ppermute(packed, "row", swap(0))
            near = exchange(near)
            fars = []
            for j in range(half):
                part = far[j * direct : (j + 1) * direct]
                fars.append(lax.ppermute(part, "row", swap(j)))
            other = (row ^ half) * grp_count + grp
            source = lax.dynamic_slice(
                everything, (other, 0, width + LANES), (1, 1, half * extra)
            ).reshape(1, half * extra).astype(jnp.int32)
            proxied = unpack(source, packed, half * extra)
            proxied = exchange(proxied)
            out = gather(near, half)
            return finish(proxied, out, fars, half, cap, direct)

        return run

    which = sum((most > size).astype(jnp.int32) for size in sizes[:-1])
    return lax.switch(
        which, [branch(size) for size in sizes],
        table, ids, everything, features,
    )


def solution(mesh):
    in_specs = (P(AXES, None), P(AXES), P(AXES, None))
    return jax.shard_map(
        body, mesh=mesh, in_specs=in_specs, out_specs=P(AXES, None, None), check_vma=False
    )
```

time: 134 us -> 132 us (0.985)
  blocking collectives: 14.8 us -> 0 us
  waiting for transfers between devices: 57.4 us -> 65.4 us
  starting transfers between devices: 33.3 us -> 40.7 us
  Pallas kernels: 17 us -> 13.7 us
    all_to_all x1 -> x0, blocking collectives: 14.8 us -> none  [body(): lax.all_to_all(tails(place, ids, owner_map, features, row_count * grp_cou...]
    all_to_all x0 -> x1, waiting for transfers between devices: none -> 7.4 us  [body(): lax.all_to_all(message, AXES, split_axis=0, concat_axis=0, tiled=True)]
    all_to_all x0 -> x1, starting transfers between devices: none -> 7.33 us  [body(): lax.all_to_all(message, AXES, split_axis=0, concat_axis=0, tiled=True)]
    pallas_call x3, Pallas kernels: 8.31 us -> 6.76 us  [the longest x1 2.99 us: tails(): pl.pallas_call(functools.partial(tail_kernel, row_count=row_count, cap=ca...]
    cond x26 -> x24, local copies, waits for them, and re-layouts: 7.74 us -> 8.72 us
  transfers between devices with their start and end apart: 11 -> 12, of which waited for: 7 -> 8; matrix products, arithmetic and copies ran while one was open for 1% -> 1% of each run, Pallas kernels for 3% -> 3%
where the time goes in v4:
time: 132 us; the launch traced here: 131 us
  waiting for transfers between devices  65.4 us (50%)
  starting transfers between devices  40.7 us (31%)
  Pallas kernels  13.7 us (10%)
  local copies, waits for them, and re-layouts  10.1 us (8%)
    ppermute x1, waiting for transfers between devices, run(): packed = lax.ppermute(packed, 'row', swap(0))  32.3 us
    ppermute x8, waiting for transfers between devices, run(): fars.append(lax.ppermute(part, 'row', swap(j)))  25.7 us
    ppermute x8, starting transfers between devices, run(): fars.append(lax.ppermute(part, 'row', swap(j)))  21.1 us
    all_to_all x2, starting transfers between devices, exchange(): lax.all_to_all(x, 'row', split_axis=0, concat_axis=0, tiled=True, axis_in...  11.5 us
    cond x24, local copies, waits for them, and re-layouts  8.72 us
    all_to_all x1, waiting for transfers between devices, body(): lax.all_to_all(message, AXES, split_axis=0, concat_axis=0, tiled=True)  7.4 us
    all_to_all x1, starting transfers between devices, body(): lax.all_to_all(message, AXES, split_axis=0, concat_axis=0, tiled=True)  7.33 us
    pallas_call x1, Pallas kernels, slotted(): pl.pallas_call(functools.partial(blocks_kernel, owner_count=owner_count,...  5.6 us
  transfers between devices with their start and end apart: 12, of which 8 were waited for; matrix products, arithmetic and copies ran while one was open for 1% of the time, Pallas kernels for 3%

profile of v4, /device:TPU:0, one launch (start us, length us, event | category | flops | bytes accessed | tf_op | source)
XLA Modules:
  0.0 131.4 jit_solution(4802951812583156506)
XLA Ops:
  0.0 3.0 %tails.1 = (f32[32,1,512]{2,1,0:T(1,128)}, s32[3,128]{1,0:T(4,128)S(1)}) custom-call(s32[32,128]{1,0:T(8,128)} %bitcast.13, s32[1,64]{1,0:T(1,128)} %owners_hbm.1, f32[4096,256]{1,0:T(8,128)} %x_hbm.1), custom_call_target="tpu_custom_call" | custom-call | tf_op jit(solution)/shard_map/tails/pallas_call | solution.py:115
  3.0 7.3 %all-to-all-start.12 = ((f32[32,1,512]{2,1,0:T(1,128)}), f32[32,1,512]{2,1,0:T(1,128)S(1)}, u32[]{:S(2)}, u32[]{:S(2)}) async-start(f32[32,1,512]{2,1,0:T(1,128)} %get-tuple-element.140), calls=%async_computation.12 | async-start | bytes 131072 | tf_op jit(solution)/shard_map/all_to_all | solution.py:381
  10.3 7.4 %all-to-all-done.12 = f32[32,1,512]{2,1,0:T(1,128)S(1)} async-done(((f32[32,1,512]{2,1,0:T(1,128)}), f32[32,1,512]{2,1,0:T(1,128)S(1)}, u32[]{:S(2)}, u32[]{:S(2)}) %all-to-all-start.12) | async-done | bytes 65568 | tf_op jit(solution)/shard_map/all_to_all | solution.py:381
  17.8 0.7 slice_reduce_fusion
  19.1 0.0 copy-done.71
  19.1 112.3 %conditional.1 = (bf16[128,64,256]{2,1,0:T(8,128)(2,1)}) conditional(s32[]{:T(128)} %clamp.3, (s32[]{:T(128)}, s32[]{:T(128)}, f32[32,1,512]{2,1,0:T(1,128)S(1)}, s32[3,128]{1,0:T(4,128)S(1)}, s32[32,128]{1,0:T(8,128)S(1)}, /*index=5*/f32[4096,256]{1,0:T(8,128)}) %tuple.78, (s32[]{:T(128)}, s32[]{:T(128)}, ...), branch_computations={%region_1.0_spmd, %region_2.0_spmd, %region_3.0_spmd, %region_4.0_... | conditional | flops 38 | bytes 30671974 | solution.py:422
  19.2 5.6 %slotted.6 = (bf16[64,64,256]{2,1,0:T(8,128)(2,1)}, bf16[32,64,256]{2,1,0:T(8,128)(2,1)}, bf16[14,64,256]{2,1,0:T(8,128)(2,1)}) custom-call(s32[3,128]{1,0:T(4,128)S(1)} %get-tuple-element.86.table_hbm, s32[32,128]{1,0:T(8,128)S(1)} %get-tuple-element.88.ids_hbm, f32[32,1,512]{2,1,0:T(1,128)S(1)} %get-tuple-element.74.all_hbm, ...), custom_call_target="tpu_custom_call" | custom-call | tf_op jit(solution)/shard_map/cond/branch_0_fun/slotted/pallas_call | solution.py:252
  24.8 0.0 copy-start.75
  24.8 3.7 %all-to-all-start.1 = ((bf16[64,64,256]{2,1,0:T(8,128)(2,1)}), bf16[64,64,256]{2,1,0:T(8,128)(2,1)S(1)}, u32[]{:S(2)}, u32[]{:S(2)}) async-start(bf16[64,64,256]{2,1,0:T(8,128)(2,1)} %get-tuple-element.91), calls=%async_computation.1 | async-start | bytes 4194304 | tf_op jit(solution)/shard_map/cond/branch_0_fun/all_to_all | solution.py:395
  28.5 0.0 copy-done.75
  28.5 0.8 collective-permute-start
  29.3 32.3 %collective-permute-done.packed_ref = bf16[14,64,256]{2,1,0:T(8,128)(2,1)S(1)} collective-permute-done((bf16[14,64,256]{2,1,0:T(8,128)(2,1)S(1)}, bf16[14,64,256]{2,1,0:T(8,128)(2,1)S(1)}, u32[]{:S(2)}, u32[]{:S(2)}) %collective-permute-start) | collective-permute-done | bytes 458784 | tf_op jit(solution)/shard_map/cond/branch_0_fun/ppermute | solution.py:404
  61.6 2.4 %unpack.6 = bf16[32,64,256]{2,1,0:T(8,128)(2,1)S(1)} custom-call(s32[1,32]{1,0:T(1,128)S(1)} %convert_bitcast_fusion.source_ref, bf16[14,64,256]{2,1,0:T(8,128)(2,1)S(1)} %collective-permute-done.packed_ref), custom_call_target="tpu_custom_call" | custom-call | tf_op jit(solution)/shard_map/cond/branch_0_fun/unpack/pallas_call | solution.py:293
  64.1 0.0 copy-start.3
  64.1 1.0 copy-done.3
  65.1 0.0 all-to-all-done.1.near_ref
  65.1 7.7 %all-to-all-start = ((bf16[32,64,256]{2,1,0:T(8,128)(2,1)}), bf16[32,64,256]{2,1,0:T(8,128)(2,1)S(1)}, u32[]{:S(2)}, u32[]{:S(2)}) async-start(bf16[32,64,256]{2,1,0:T(8,128)(2,1)} %copy-done.3), calls=%async_computation | async-start | bytes 2097152 | tf_op jit(solution)/shard_map/cond/branch_0_fun/all_to_all | solution.py:395
  72.8 1.4 %fusion = (bf16[4,64,256]{2,1,0:T(8,128)(2,1)S(1)}, bf16[4,64,256]{2,1,0:T(8,128)(2,1)S(1)}, bf16[4,64,256]{2,1,0:T(8,128)(2,1)S(1)}, bf16[4,64,256]{2,1,0:T(8,1...) fusion(bf16[32,64,256]{2,1,0:T(8,128)(2,1)} %get-tuple-element.92), kind=kLoop, calls=%fused_computation.7 | loop fusion | bytes 2097152 | tf_op jit(solution)/shard_map/cond/branch_0_fun/slice | solution.py:408
  74.2 6.3 %collective-permute-start.8 = (bf16[4,64,256]{2,1,0:T(8,128)(2,1)S(1)}, bf16[4,64,256]{2,1,0:T(8,128)(2,1)S(1)}, u32[]{:S(2)}, u32[]{:S(2)}) collective-permute-start(bf16[4,64,256]{2,1,0:T(8,128)(2,1)S(1)} %get-tuple-element.143), channel_id=1, source_target_pairs={{0,30},{2,28},{4,26},{6,24},{8,22},{10,20},{12,18},{14,16},{16,14}... | collective-permute-start | bytes 393224 | tf_op jit(solution)/shard_map/cond/branch_0_fun/ppermute | solution.py:409
  80.4 0.0 collective-permute-start.7
  80.4 3.8 %collective-permute-start.6 = (bf16[4,64,256]{2,1,0:T(8,128)(2,1)S(1)}, bf16[4,64,256]{2,1,0:T(8,128)(2,1)S(1)}, u32[]{:S(2)}, u32[]{:S(2)}) collective-permute-start(bf16[4,64,256]{2,1,0:T(8,128)(2,1)S(1)} %get-tuple-element.145), channel_id=1, source_target_pairs={{0,26},{2,24},{4,30},{6,28},{8,18},{10,16},{12,22},{14,20},{16,10}... | collective-permute-start | bytes 393224 | tf_op jit(solution)/shard_map/cond/branch_0_fun/ppermute | solution.py:409
  84.3 0.1 collective-permute-start.5
  84.3 1.0 collective-permute-start.4
  85.4 10.9 %collective-permute-done.8.refs_7_ = bf16[4,64,256]{2,1,0:T(8,128)(2,1)S(1)} collective-permute-done((bf16[4,64,256]{2,1,0:T(8,128)(2,1)S(1)}, bf16[4,64,256]{2,1,0:T(8,128)(2,1)S(1)}, u32[]{:S(2)}, u32[]{:S(2)}) %collective-permute-start.8) | collective-permute-done | bytes 131104 | tf_op jit(solution)/shard_map/cond/branch_0_fun/ppermute | solution.py:409
  96.3 0.0 collective-permute-start.3
  96.3 3.5 %collective-permute-done.7.refs_6_ = bf16[4,64,256]{2,1,0:T(8,128)(2,1)S(1)} collective-permute-done((bf16[4,64,256]{2,1,0:T(8,128)(2,1)S(1)}, bf16[4,64,256]{2,1,0:T(8,128)(2,1)S(1)}, u32[]{:S(2)}, u32[]{:S(2)}) %collective-permute-start.7) | collective-permute-done | bytes 131104 | tf_op jit(solution)/shard_map/cond/branch_0_fun/ppermute | solution.py:409
  99.8 0.0 collective-permute-start.2
  99.8 1.2 collective-permute-done.6.refs_5_
  101.0 9.9 %collective-permute-start.1 = (bf16[4,64,256]{2,1,0:T(8,128)(2,1)S(1)}, bf16[4,64,256]{2,1,0:T(8,128)(2,1)S(1)}, u32[]{:S(2)}, u32[]{:S(2)}) collective-permute-start(bf16[4,64,256]{2,1,0:T(8,128)(2,1)S(1)} %get-tuple-element.150), channel_id=1, source_target_pairs={{0,16},{2,18},{4,20},{6,22},{8,24},{10,26},{12,28},{14,30},{16,0},... | collective-permute-start | bytes 393224 | tf_op jit(solution)/shard_map/cond/branch_0_fun/ppermute | solution.py:409
  110.9 1.3 %gather.6.part_ref = bf16[128,64,256]{2,1,0:T(8,128)(2,1)} custom-call(bf16[64,64,256]{2,1,0:T(8,128)(2,1)S(1)} %all-to-all-done.1.near_ref), custom_call_target="tpu_custom_call" | custom-call | tf_op jit(solution)/shard_map/cond/branch_0_fun/gather/pallas_call | solution.py:317
  112.2 0.0 collective-permute-done.5.refs_4_
  112.2 0.0 copy-start.6
  112.2 0.6 copy-done.6
  112.9 6.4 %collective-permute-done.4.refs_3_ = bf16[4,64,256]{2,1,0:T(8,128)(2,1)S(1)} collective-permute-done((bf16[4,64,256]{2,1,0:T(8,128)(2,1)S(1)}, bf16[4,64,256]{2,1,0:T(8,128)(2,1)S(1)}, u32[]{:S(2)}, u32[]{:S(2)}) %collective-permute-start.4) | collective-permute-done | bytes 131104 | tf_op jit(solution)/shard_map/cond/branch_0_fun/ppermute | solution.py:409
  119.3 0.6 copy-done.18
  119.9 2.3 %collective-permute-done.3.refs_2_ = bf16[4,64,256]{2,1,0:T(8,128)(2,1)S(1)} collective-permute-done((bf16[4,64,256]{2,1,0:T(8,128)(2,1)S(1)}, bf16[4,64,256]{2,1,0:T(8,128)(2,1)S(1)}, u32[]{:S(2)}, u32[]{:S(2)}) %collective-permute-start.3) | collective-permute-done | bytes 131104 | tf_op jit(solution)/shard_map/cond/branch_0_fun/ppermute | solution.py:409
  122.2 0.7 copy-done.30
  122.8 1.4 %collective-permute-done.2.refs_1_ = bf16[4,64,256]{2,1,0:T(8,128)(2,1)S(1)} collective-permute-done((bf16[4,64,256]{2,1,0:T(8,128)(2,1)S(1)}, bf16[4,64,256]{2,1,0:T(8,128)(2,1)S(1)}, u32[]{:S(2)}, u32[]{:S(2)}) %collective-permute-start.2) | collective-permute-done | bytes 131104 | tf_op jit(solution)/shard_map/cond/branch_0_fun/ppermute | solution.py:409
  124.3 0.7 copy-done.42
  124.9 0.0 collective-permute-done.1.refs_0_
  124.9 0.6 copy-done.54
  125.6 0.0 all-to-all-done.proxied_ref
  125.6 0.9 copy-done.7
  126.5 0.9 copy-done.19
  127.4 0.9 copy-done.31
  128.3 0.9 copy-done.43
  129.2 0.9 copy-done.55
  130.1 1.3 finish.6
  (11 shorter events, 0.0 us)
Async XLA Ops:
  0.0 19.1 %copy-start.71 = (s32[4096]{0:T(1024)S(1)}, s32[4096]{0:T(1024)}, u32[]{:S(2)}) copy-start(s32[4096]{0:T(1024)} %param.10) | copy-start | bytes 49156
  3.0 14.7 %all-to-all-start.12 = ((f32[32,1,512]{2,1,0:T(1,128)}), f32[32,1,512]{2,1,0:T(1,128)S(1)}, u32[]{:S(2)}, u32[]{:S(2)}) async-start(f32[32,1,512]{2,1,0:T(1,128)} %get-tuple-element.140), calls=%async_computation.12 | async-start | bytes 131072 | tf_op jit(solution)/shard_map/all_to_all | solution.py:381
  24.8 3.8 %copy-start.75 = (bf16[14,64,256]{2,1,0:T(8,128)(2,1)S(1)}, bf16[14,64,256]{2,1,0:T(8,128)(2,1)}, u32[]{:S(2)}) copy-start(bf16[14,64,256]{2,1,0:T(8,128)(2,1)} %get-tuple-element.90) | copy-start | bytes 1376260 | tf_op jit(solution)/shard_map/cond
  24.8 40.3 %all-to-all-start.1 = ((bf16[64,64,256]{2,1,0:T(8,128)(2,1)}), bf16[64,64,256]{2,1,0:T(8,128)(2,1)S(1)}, u32[]{:S(2)}, u32[]{:S(2)}) async-start(bf16[64,64,256]{2,1,0:T(8,128)(2,1)} %get-tuple-element.91), calls=%async_computation.1 | async-start | bytes 4194304 | tf_op jit(solution)/shard_map/cond/branch_0_fun/all_to_all | solution.py:395
  28.5 33.1 %collective-permute-start = (bf16[14,64,256]{2,1,0:T(8,128)(2,1)S(1)}, bf16[14,64,256]{2,1,0:T(8,128)(2,1)S(1)}, u32[]{:S(2)}, u32[]{:S(2)}) collective-permute-start(bf16[14,64,256]{2,1,0:T(8,128)(2,1)S(1)} %copy-done.75), channel_id=1, source_target_pairs={{0,16},{2,18},{4,20},{6,22},{8,24},{10,26},{12,28},{14,30},{16,0},... | collective-permute-start | bytes 1376264 | tf_op jit(solution)/shard_map/cond/branch_0_fun/ppermute | solution.py:404
  64.1 1.0 copy-start.3
  65.1 60.5 %all-to-all-start = ((bf16[32,64,256]{2,1,0:T(8,128)(2,1)}), bf16[32,64,256]{2,1,0:T(8,128)(2,1)S(1)}, u32[]{:S(2)}, u32[]{:S(2)}) async-start(bf16[32,64,256]{2,1,0:T(8,128)(2,1)} %copy-done.3), calls=%async_computation | async-start | bytes 2097152 | tf_op jit(solution)/shard_map/cond/branch_0_fun/all_to_all | solution.py:395
  74.2 22.2 %collective-permute-start.8 = (bf16[4,64,256]{2,1,0:T(8,128)(2,1)S(1)}, bf16[4,64,256]{2,1,0:T(8,128)(2,1)S(1)}, u32[]{:S(2)}, u32[]{:S(2)}) collective-permute-start(bf16[4,64,256]{2,1,0:T(8,128)(2,1)S(1)} %get-tuple-element.143), channel_id=1, source_target_pairs={{0,30},{2,28},{4,26},{6,24},{8,22},{10,20},{12,18},{14,16},{16,14}... | collective-permute-start | bytes 393224 | tf_op jit(solution)/shard_map/cond/branch_0_fun/ppermute | solution.py:409
  80.4 19.4 %collective-permute-start.7 = (bf16[4,64,256]{2,1,0:T(8,128)(2,1)S(1)}, bf16[4,64,256]{2,1,0:T(8,128)(2,1)S(1)}, u32[]{:S(2)}, u32[]{:S(2)}) collective-permute-start(bf16[4,64,256]{2,1,0:T(8,128)(2,1)S(1)} %get-tuple-element.144), channel_id=1, source_target_pairs={{0,28},{2,30},{4,24},{6,26},{8,20},{10,22},{12,16},{14,18},{16,12}... | collective-permute-start | bytes 393224 | tf_op jit(solution)/shard_map/cond/branch_0_fun/ppermute | solution.py:409
  80.4 20.6 %collective-permute-start.6 = (bf16[4,64,256]{2,1,0:T(8,128)(2,1)S(1)}, bf16[4,64,256]{2,1,0:T(8,128)(2,1)S(1)}, u32[]{:S(2)}, u32[]{:S(2)}) collective-permute-start(bf16[4,64,256]{2,1,0:T(8,128)(2,1)S(1)} %get-tuple-element.145), channel_id=1, source_target_pairs={{0,26},{2,24},{4,30},{6,28},{8,18},{10,16},{12,22},{14,20},{16,10}... | collective-permute-start | bytes 393224 | tf_op jit(solution)/shard_map/cond/branch_0_fun/ppermute | solution.py:409
  84.3 28.0 %collective-permute-start.5 = (bf16[4,64,256]{2,1,0:T(8,128)(2,1)S(1)}, bf16[4,64,256]{2,1,0:T(8,128)(2,1)S(1)}, u32[]{:S(2)}, u32[]{:S(2)}) collective-permute-start(bf16[4,64,256]{2,1,0:T(8,128)(2,1)S(1)} %get-tuple-element.146), channel_id=1, source_target_pairs={{0,24},{2,26},{4,28},{6,30},{8,16},{10,18},{12,20},{14,22},{16,8},... | collective-permute-start | bytes 393224 | tf_op jit(solution)/shard_map/cond/branch_0_fun/ppermute | solution.py:409
  84.3 34.9 %collective-permute-start.4 = (bf16[4,64,256]{2,1,0:T(8,128)(2,1)S(1)}, bf16[4,64,256]{2,1,0:T(8,128)(2,1)S(1)}, u32[]{:S(2)}, u32[]{:S(2)}) collective-permute-start(bf16[4,64,256]{2,1,0:T(8,128)(2,1)S(1)} %get-tuple-element.147), channel_id=1, source_target_pairs={{0,22},{2,20},{4,18},{6,16},{8,30},{10,28},{12,26},{14,24},{16,6},... | collective-permute-start | bytes 393224 | tf_op jit(solution)/shard_map/cond/branch_0_fun/ppermute | solution.py:409
  96.3 25.9 %collective-permute-start.3 = (bf16[4,64,256]{2,1,0:T(8,128)(2,1)S(1)}, bf16[4,64,256]{2,1,0:T(8,128)(2,1)S(1)}, u32[]{:S(2)}, u32[]{:S(2)}) collective-permute-start(bf16[4,64,256]{2,1,0:T(8,128)(2,1)S(1)} %get-tuple-element.148), channel_id=1, source_target_pairs={{0,20},{2,22},{4,16},{6,18},{8,28},{10,30},{12,24},{14,26},{16,4},... | collective-permute-start | bytes 393224 | tf_op jit(solution)/shard_map/cond/branch_0_fun/ppermute | solution.py:409
  99.8 24.5 %collective-permute-start.2 = (bf16[4,64,256]{2,1,0:T(8,128)(2,1)S(1)}, bf16[4,64,256]{2,1,0:T(8,128)(2,1)S(1)}, u32[]{:S(2)}, u32[]{:S(2)}) collective-permute-start(bf16[4,64,256]{2,1,0:T(8,128)(2,1)S(1)} %get-tuple-element.149), channel_id=1, source_target_pairs={{0,18},{2,16},{4,22},{6,20},{8,26},{10,24},{12,30},{14,28},{16,2},... | collective-permute-start | bytes 393224 | tf_op jit(solution)/shard_map/cond/branch_0_fun/ppermute | solution.py:409
  101.0 23.9 %collective-permute-start.1 = (bf16[4,64,256]{2,1,0:T(8,128)(2,1)S(1)}, bf16[4,64,256]{2,1,0:T(8,128)(2,1)S(1)}, u32[]{:S(2)}, u32[]{:S(2)}) collective-permute-start(bf16[4,64,256]{2,1,0:T(8,128)(2,1)S(1)} %get-tuple-element.150), channel_id=1, source_target_pairs={{0,16},{2,18},{4,20},{6,22},{8,24},{10,26},{12,28},{14,30},{16,0},... | collective-permute-start | bytes 393224 | tf_op jit(solution)/shard_map/cond/branch_0_fun/ppermute | solution.py:409
  112.2 0.6 copy-start.6
  119.3 0.6 copy-start.18
  122.2 0.7 copy-start.30
  124.3 0.7 copy-start.42
  124.9 0.6 copy-start.54
  125.6 0.9 copy-start.7
  126.5 0.9 copy-start.19
  127.4 0.9 copy-start.31
  128.3 0.9 copy-start.43
  129.2 0.9 copy-start.55
